TPU v7x, 128 devices: a whole 4x4x4 slice. The times are simulated.
128 devices in a mesh: tile: 64 (over z, y, x), depth: 2 (over core).
Axes of the slice: x: 4, y: 4, z: 4, core: 2. Of those that a mesh axis runs over, the one named last changes fastest.
Arguments:
- transmission: float32 [2, 2, 1024, 8192], P('depth', None, None, 'tile'), may hold values from -4.2 to 4.2
- probe_modes: float32 [6, 2, 256, 256], replicated, may hold values from -6 to 6
- measured: float32 [256, 256, 256], P('tile'), may hold values from 1 to 30
- scan_rows: int32 [256], P('tile'), may hold values from 0 to 768
- scan_cols: int32 [256], P('tile'), may hold values from 0 to 127
- counts: int32 [64], P('tile'), may hold values from 1 to 4, as said below
- dataset: int32 [256], P('tile'), may hold values from 0 to 15
- dose_scale: float32 [16], replicated, may hold values from 0.5 to 2
- background: float32 [16], replicated, may hold values from 0.5 to 8
Outputs:
- object_grad: float32 [2, 2, 1024, 8192], P('depth', None, None, 'tile')
Inputs may be any that keep to these rules, and one draw needn't show every extreme that they name: Tile t's valid positions are its first counts[t] slots; the other slots' rows, columns, datasets and intensities are ignored. Some tile has all 4 slots valid.
All inputs are finite; a program needn't handle non-finite values.
Results may differ from a plain program's by a relative error of at most 0.011.
Values may be sent and summed in bfloat16 or wider, within the bound.
A program may use at most 128 MiB of HBM per device.

v0:
```python
import math

import jax
import jax.numpy as jnp
from jax import lax
from jax.sharding import PartitionSpec as P


def padded(block, sides, width):
    for axis, dim in sides:
        count = lax.axis_size(axis)
        forward = [(i, i + 1) for i in range(count - 1)]
        backward = [(target, source) for source, target in forward]
        low = lax.ppermute(
            lax.slice_in_dim(block, block.shape[dim] - width, None, axis=dim), axis, forward
        )
        high = lax.ppermute(lax.slice_in_dim(block, 0, width, axis=dim), axis, backward)
        block = jnp.concatenate([low, block, high], axis=dim)
    return block


def shifted(block, axis, distance):
    devices = range(lax.axis_size(axis))
    route = [(i - distance, i) for i in devices if i - distance in devices]
    return lax.ppermute(block, axis, route)


def times_complex(first, second):
    first_re = first[..., 0, :, :]
    first_im = first[..., 1, :, :]
    second_re = second[..., 0, :, :]
    second_im = second[..., 1, :, :]
    return jnp.stack(
        [first_re * second_re - first_im * second_im, first_re * second_im + first_im * second_re],
        axis=-3,
    )


def times_conjugate(first, second):
    first_re = first[..., 0, :, :]
    first_im = first[..., 1, :, :]
    second_re = second[..., 0, :, :]
    second_im = second[..., 1, :, :]
    return jnp.stack(
        [first_re * second_re + first_im * second_im, first_re * second_im - first_im * second_re],
        axis=-3,
    )


def block_table(real_part, imag_part):
    upper = jnp.stack([real_part, -imag_part])
    lower = jnp.stack([imag_part, real_part])
    return jnp.stack([upper, lower]).astype(jnp.bfloat16)


def fresnel_tables(length):
    counter = jnp.arange(length, dtype=jnp.int32)
    product = counter[:, None] * counter[None, :] % length
    angles = 2.0 * math.pi / length * product.astype(jnp.float32)
    scaling = 1.0 / math.sqrt(length)
    dft_re = jnp.cos(angles) * scaling
    dft_im = -jnp.sin(angles) * scaling
    signed = jnp.where(counter < length // 2, counter, counter - length)
    phases = -math.pi / length * (signed * signed % (2 * length)).astype(jnp.float32)
    filter_re = jnp.cos(phases)[:, None]
    filter_im = jnp.sin(phases)[:, None]
    mixed_re = filter_re * dft_re - filter_im * dft_im
    mixed_im = filter_re * dft_im + filter_im * dft_re
    highest = lax.Precision.HIGHEST
    kernel_re = jnp.dot(dft_re, mixed_re, precision=highest) + jnp.dot(
        dft_im, mixed_im, precision=highest
    )
    kernel_im = jnp.dot(dft_re, mixed_im, precision=highest) - jnp.dot(
        dft_im, mixed_re, precision=highest
    )
    return (
        block_table(dft_re, dft_im),
        block_table(dft_re, -dft_im),
        block_table(kernel_re, kernel_im),
        block_table(kernel_re, -kernel_im),
    )


def apply_sides(table, waves):
    inner = jnp.einsum("cdij,bdjk->bcik", table, waves, preferred_element_type=jnp.float32).astype(
        jnp.bfloat16
    )
    return jnp.einsum("bdij,cdjk->bcik", inner, table, preferred_element_type=jnp.float32)


def far_gradient(far_field, measured, validity, scales, offsets):
    intensity = (
        scales[:, None, None] * jnp.sum(far_field * far_field, axis=(1, 2)) + offsets[:, None, None]
    )
    factor = (validity * scales)[:, None, None] * (1.0 - jnp.sqrt(measured) / jnp.sqrt(intensity))
    return (factor[:, None, None] * far_field).astype(jnp.bfloat16)


def add_patches(gradient, scan_rows, scan_cols, contributions):
    zero = jnp.zeros((), jnp.int32)
    length = contributions.shape[-1]

    def add_one(position, current):
        place = (zero, scan_rows[position], scan_cols[position])
        present = lax.dynamic_slice(current, place, (2, length, length))
        return lax.dynamic_update_slice(current, present + contributions[position], place)

    return lax.fori_loop(0, contributions.shape[0], add_one, gradient)


def shards(
    transmission,
    probe_modes,
    measured,
    scan_rows,
    scan_cols,
    counts,
    dataset,
    dose_scale,
    background,
):
    length = probe_modes.shape[-1]
    half_width = length // 2
    slot_count = measured.shape[0]
    tile_width = transmission.shape[-1]
    depth_count = lax.axis_size("depth")
    band_index = lax.axis_index("depth")
    zero = jnp.zeros((), jnp.int32)
    dft_table, dft_adjoint, kernel_table, kernel_adjoint = fresnel_tables(length)
    onehot = dataset[:, None] == jnp.arange(dose_scale.shape[0], dtype=jnp.int32)[None, :]
    scales = jnp.sum(jnp.where(onehot, dose_scale[None, :], 0.0), axis=1)
    offsets = jnp.sum(jnp.where(onehot, background[None, :], 0.0), axis=1)
    validity = (jnp.arange(slot_count, dtype=jnp.int32) < counts[0]).astype(jnp.float32)
    extended = padded(transmission[0], (("tile", 2),), half_width)

    def cut_patch(row_start, col_start):
        return lax.dynamic_slice(extended, (zero, row_start, col_start), (2, length, length))

    own_patches = jax.vmap(cut_patch)(scan_rows, scan_cols)
    forward_table = jnp.where(band_index == depth_count - 1, dft_table, kernel_table)
    backward_table = jnp.where(band_index == depth_count - 1, dft_adjoint, kernel_adjoint)
    wave_shape = probe_modes.shape
    section_count = slot_count + depth_count - 1

    def forward_section(section_now, loop_state):
        incoming, saved_in, saved_out = loop_state
        offset_slot = section_now - band_index
        active = (offset_slot >= 0) & (offset_slot < slot_count)
        chosen = jnp.clip(offset_slot, 0, slot_count - 1)
        wave_in = jnp.where(band_index == 0, probe_modes, incoming.astype(jnp.float32))
        patch_now = lax.dynamic_index_in_dim(own_patches, chosen, 0, keepdims=False)

        def forward_compute(saved_pair):
            applied = times_complex(wave_in, patch_now[None]).astype(jnp.bfloat16)
            result = apply_sides(forward_table, applied)
            stored_in = lax.dynamic_update_index_in_dim(saved_pair[0], wave_in, chosen, 0)
            stored_out = lax.dynamic_update_index_in_dim(saved_pair[1], result, chosen, 0)
            return ((stored_in, stored_out), result)

        def forward_pass_through(saved_pair):
            return (saved_pair, jnp.zeros(wave_shape, jnp.float32))

        (saved_in, saved_out), result = lax.cond(
            active, forward_compute, forward_pass_through, (saved_in, saved_out)
        )
        incoming = shifted(result.astype(jnp.bfloat16), "depth", 1)
        return (incoming, saved_in, saved_out)

    stored = jnp.zeros((slot_count,) + wave_shape, jnp.float32)
    start_state = (jnp.zeros(wave_shape, jnp.bfloat16), stored, stored)
    _, saved_in, saved_out = lax.fori_loop(0, section_count, forward_section, start_state)
    far_grads = far_gradient(saved_out, measured, validity, scales, offsets)

    def backward_section(section_now, loop_state):
        incoming, saved_back = loop_state
        offset_slot = section_now - (depth_count - 1 - band_index)
        active = (offset_slot >= 0) & (offset_slot < slot_count)
        chosen = jnp.clip(offset_slot, 0, slot_count - 1)
        far_now = lax.dynamic_index_in_dim(far_grads, chosen, 0, keepdims=False)
        grad_in = jnp.where(band_index == depth_count - 1, far_now, incoming)
        patch_now = lax.dynamic_index_in_dim(own_patches, chosen, 0, keepdims=False)

        def backward_compute(saved_grads):
            back_wave = apply_sides(backward_table, grad_in)
            sendback = times_conjugate(patch_now[None], back_wave).astype(jnp.bfloat16)
            return (lax.dynamic_update_index_in_dim(saved_grads, back_wave, chosen, 0), sendback)

        def backward_pass_through(saved_grads):
            return (saved_grads, jnp.zeros(wave_shape, jnp.bfloat16))

        saved_back, sendback = lax.cond(active, backward_compute, backward_pass_through, saved_back)
        incoming = shifted(sendback, "depth", -1)
        return (incoming, saved_back)

    _, saved_back = lax.fori_loop(
        0, section_count, backward_section, (jnp.zeros(wave_shape, jnp.bfloat16), stored)
    )
    contributions = jnp.sum(times_conjugate(saved_in, saved_back), axis=1)
    gradient = add_patches(
        jnp.zeros(extended.shape, jnp.float32), scan_rows, scan_cols, contributions
    )
    from_left = shifted(
        gradient[:, :, tile_width + half_width :].astype(jnp.bfloat16), "tile", 1
    ).astype(jnp.float32)
    from_right = shifted(gradient[:, :, :half_width].astype(jnp.bfloat16), "tile", -1).astype(
        jnp.float32
    )
    own_part = gradient[:, :, half_width : half_width + tile_width]
    own_part = own_part.at[:, :, :half_width].add(from_left)
    own_part = own_part.at[:, :, tile_width - half_width :].add(from_right)
    return own_part[None]


def solution(mesh):
    in_specs = (
        P("depth", None, None, "tile"),
        P(),
        P("tile", None, None),
        P("tile"),
        P("tile"),
        P("tile"),
        P("tile"),
        P(),
        P(),
    )
    out_specs = P("depth", None, None, "tile")
    return jax.shard_map(shards, mesh=mesh, in_specs=in_specs, out_specs=out_specs, check_vma=False)
```

profile of v0, /device:TPU:96, one launch (start us, length us, event | category | flops | bytes accessed | tf_op | source)
XLA Modules:
  0.0 343.4 jit_solution(1036185877871404567)
XLA Ops:
  0.0 3.5 %collective-permute-start.2 = (f32[2,1024,128]{2,1,0:T(8,128)}, f32[2,1024,128]{2,1,0:T(8,128)S(1)}, u32[]{:S(2)}, u32[]{:S(2)}) collective-permute-start(f32[2,1024,128]{2,1,0:T(8,128)} %bitcast.162), channel_id=1, source_target_pairs={{0,2},{2,4},{4,6},{6,8},{8,10},{10,12},{12,14},{14,16},{16,18},{18... | collective-permute-start | bytes 3145736 | tf_op jit(solution)/shard_map/ppermute | solution.py:14
  3.6 6.7 %collective-permute-start.3 = (f32[2,1024,128]{2,1,0:T(8,128)}, f32[2,1024,128]{2,1,0:T(8,128)}, u32[]{:S(2)}, u32[]{:S(2)}) collective-permute-start(f32[2,1024,128]{2,1,0:T(8,128)} %bitcast.163), channel_id=1, source_target_pairs={{2,0},{4,2},{6,4},{8,6},{10,8},{12,10},{14,12},{16,14},{18,16},{20... | collective-permute-start | bytes 3145736 | tf_op jit(solution)/shard_map/ppermute | solution.py:17
  21.7 9.7 %collective-permute-done.2 = f32[2,1024,128]{2,1,0:T(8,128)S(1)} collective-permute-done((f32[2,1024,128]{2,1,0:T(8,128)}, f32[2,1024,128]{2,1,0:T(8,128)S(1)}, u32[]{:S(2)}, u32[]{:S(2)}) %collective-permute-start.2) | collective-permute-done | bytes 1048608 | tf_op jit(solution)/shard_map/ppermute | solution.py:14
  32.7 1.7 pad_maximum_fusion.1
  34.4 11.9 %while.59 = (s32[]{:T(128)}, f32[2,1024,384]{2,1,0:T(8,128)S(1)}, s32[4,3]{1,0:T(4,128)S(1)}, f32[4,2,256,256]{3,2,1,0:T(8,128)}, s32[]{:T(128)}) while((s32[]{:T(128)}, f32[2,1024,384]{2,1,0:T(8,128)S(1)}, s32[4,3]{1,0:T(4,128)S(1)}, f32[4,2,256,256]{3,2,1,0:T(8,128)}, s32[]{:T(128)}) %tuple.186), condition=%wide.while_cond.2, body=%wide.while_body.2.sunk | while | flops 2 | bytes 1050217 | solution.py:137
  35.3 2.3 bitcast_dynamic-update-slice_fusion.5
  38.2 2.3 bitcast_dynamic-update-slice_fusion.5
  41.1 2.3 bitcast_dynamic-update-slice_fusion.5
  44.1 2.3 bitcast_dynamic-update-slice_fusion.5
  46.4 6.0 %broadcast_in_dim.69.clone = f32[4,6,2,256,256]{4,3,2,1,0:T(8,128)} broadcast(f32[]{:T(128)} %constant.277.clone.1), dimensions={} | broadcast | bytes 12582916 | tf_op jit(solution)/shard_map/broadcast_in_dim | solution.py:169
  52.4 6.0 %broadcast_in_dim.69.clone.1 = f32[4,6,2,256,256]{4,3,2,1,0:T(8,128)} broadcast(f32[]{:T(128)} %constant.277.clone.1), dimensions={} | broadcast | bytes 12582916 | tf_op jit(solution)/shard_map/broadcast_in_dim | solution.py:169
  59.8 94.0 %while.56 = (s32[]{:T(128)}, bf16[6,2,256,256]{3,2,1,0:T(8,128)(2,1)}, f32[4,6,2,256,256]{4,3,2,1,0:T(8,128)}, f32[4,6,2,256,256]{4,3,2,1,0:T(8,128)}, s32[]{:T(...) while((s32[]{:T(128)}, ...), condition=%wide.region_3.4_spmd, body=%wide.region_0.3_spmd.sunk | while | flops 1620049920 | bytes 37225336 | solution.py:171
  59.8 12.9 %conditional.4 = (f32[4,6,2,256,256]{4,3,2,1,0:T(8,128)}, f32[4,6,2,256,256]{4,3,2,1,0:T(8,128)}, bf16[6,2,256,256]{3,2,1,0:T(8,128)(2,1)}) conditional(s32[]{:T(128)} %convert_element_type.228, (f32[4,6,2,256,256]{4,3,2,1,0:T(8,128)}, f32[4,6,2,256,256]{4,3,2,1,0:T(8,128)}) %tuple.175, (pred[]{:T(512)}, bf16[6,2,256,256]{3,2,1,0:T(8,128)(2,1)}, ...), branch_computations={%region_1.1_spmd, %region_2.2_spmd} | conditional | flops 1620049920 | bytes 24642124 | solution.py:163
  59.8 4.7 %bitcast_dynamic-update-slice_fusion.1 = (f32[4,6,2,256,256]{4,3,2,1,0:T(8,128)}, f32[6,2,256,256]{3,2,1,0:T(8,128)S(1)}) fusion(f32[4,6,2,256,256]{4,3,2,1,0:T(8,128)} %get-tuple-element.636, s32[]{:T(128)S(6)} %min.20, f32[6,2,256,256]{3,2,1,0:T(8,128)} %get-tuple-element.638, bf16[6,2,256,256]{3,2,1,0:T(8,128)(2,1)} %get-tuple-element.639, ...), kind=kLoop, calls=%fused_computation.2 | loop fusion | flops 1572864 | bytes 11010564 | tf_op jit(solution)/shard_map/while/body/eval_jaxpr/cond/branch_1_fun/jit(dynamic_update_index_in_dim)/dynamic_update_slice | solution.py:156
  65.5 1.6 subtract_convert_fusion
  67.2 5.6 %bitcast_dynamic-update-slice_fusion = (f32[4,6,2,256,256]{4,3,2,1,0:T(8,128)}, bf16[6,256,2,256,1]{3,1,4,2,0:T(8,128)(2,1)}) fusion(f32[4,6,2,256,256]{4,3,2,1,0:T(8,128)} %get-tuple-element.641, s32[]{:T(128)S(6)} %min.20, bf16[2,2,256,256]{3,2,1,0:T(8,128)(2,1)} %get-tuple-element.643, bf16[6,1,256,256]{3,2,1,0:T(8,128)(2,1)} %get-tuple-element.770, ...), kind=kOutput, calls=%fused_computation | convolution fusion | flops 1615331328 | bytes 7340036 | tf_op jit(solution)/shard_map/while/body/eval_jaxpr/cond/branch_1_fun/bdij,cdjk->bcik/dot_general | solution.py:88
  74.1 3.1 collective-permute-done
  78.4 13.1 %conditional.4 = (f32[4,6,2,256,256]{4,3,2,1,0:T(8,128)}, f32[4,6,2,256,256]{4,3,2,1,0:T(8,128)}, bf16[6,2,256,256]{3,2,1,0:T(8,128)(2,1)}) conditional(s32[]{:T(128)} %convert_element_type.228, (f32[4,6,2,256,256]{4,3,2,1,0:T(8,128)}, f32[4,6,2,256,256]{4,3,2,1,0:T(8,128)}) %tuple.175, (pred[]{:T(512)}, bf16[6,2,256,256]{3,2,1,0:T(8,128)(2,1)}, ...), branch_computations={%region_1.1_spmd, %region_2.2_spmd} | conditional | flops 1620049920 | bytes 24642124 | solution.py:163
  78.4 4.7 %bitcast_dynamic-update-slice_fusion.1 = (f32[4,6,2,256,256]{4,3,2,1,0:T(8,128)}, f32[6,2,256,256]{3,2,1,0:T(8,128)S(1)}) fusion(f32[4,6,2,256,256]{4,3,2,1,0:T(8,128)} %get-tuple-element.636, s32[]{:T(128)S(6)} %min.20, f32[6,2,256,256]{3,2,1,0:T(8,128)} %get-tuple-element.638, bf16[6,2,256,256]{3,2,1,0:T(8,128)(2,1)} %get-tuple-element.639, ...), kind=kLoop, calls=%fused_computation.2 | loop fusion | flops 1572864 | bytes 11010564 | tf_op jit(solution)/shard_map/while/body/eval_jaxpr/cond/branch_1_fun/jit(dynamic_update_index_in_dim)/dynamic_update_slice | solution.py:156
  84.2 1.6 subtract_convert_fusion
  85.9 5.6 %bitcast_dynamic-update-slice_fusion = (f32[4,6,2,256,256]{4,3,2,1,0:T(8,128)}, bf16[6,256,2,256,1]{3,1,4,2,0:T(8,128)(2,1)}) fusion(f32[4,6,2,256,256]{4,3,2,1,0:T(8,128)} %get-tuple-element.641, s32[]{:T(128)S(6)} %min.20, bf16[2,2,256,256]{3,2,1,0:T(8,128)(2,1)} %get-tuple-element.643, bf16[6,1,256,256]{3,2,1,0:T(8,128)(2,1)} %get-tuple-element.770, ...), kind=kOutput, calls=%fused_computation | convolution fusion | flops 1615331328 | bytes 7340036 | tf_op jit(solution)/shard_map/while/body/eval_jaxpr/cond/branch_1_fun/bdij,cdjk->bcik/dot_general | solution.py:88
  92.9 3.1 collective-permute-done
  97.2 13.1 %conditional.4 = (f32[4,6,2,256,256]{4,3,2,1,0:T(8,128)}, f32[4,6,2,256,256]{4,3,2,1,0:T(8,128)}, bf16[6,2,256,256]{3,2,1,0:T(8,128)(2,1)}) conditional(s32[]{:T(128)} %convert_element_type.228, (f32[4,6,2,256,256]{4,3,2,1,0:T(8,128)}, f32[4,6,2,256,256]{4,3,2,1,0:T(8,128)}) %tuple.175, (pred[]{:T(512)}, bf16[6,2,256,256]{3,2,1,0:T(8,128)(2,1)}, ...), branch_computations={%region_1.1_spmd, %region_2.2_spmd} | conditional | flops 1620049920 | bytes 24642124 | solution.py:163
  97.2 4.8 %bitcast_dynamic-update-slice_fusion.1 = (f32[4,6,2,256,256]{4,3,2,1,0:T(8,128)}, f32[6,2,256,256]{3,2,1,0:T(8,128)S(1)}) fusion(f32[4,6,2,256,256]{4,3,2,1,0:T(8,128)} %get-tuple-element.636, s32[]{:T(128)S(6)} %min.20, f32[6,2,256,256]{3,2,1,0:T(8,128)} %get-tuple-element.638, bf16[6,2,256,256]{3,2,1,0:T(8,128)(2,1)} %get-tuple-element.639, ...), kind=kLoop, calls=%fused_computation.2 | loop fusion | flops 1572864 | bytes 11010564 | tf_op jit(solution)/shard_map/while/body/eval_jaxpr/cond/branch_1_fun/jit(dynamic_update_index_in_dim)/dynamic_update_slice | solution.py:156
  103.0 1.6 subtract_convert_fusion
  104.7 5.6 %bitcast_dynamic-update-slice_fusion = (f32[4,6,2,256,256]{4,3,2,1,0:T(8,128)}, bf16[6,256,2,256,1]{3,1,4,2,0:T(8,128)(2,1)}) fusion(f32[4,6,2,256,256]{4,3,2,1,0:T(8,128)} %get-tuple-element.641, s32[]{:T(128)S(6)} %min.20, bf16[2,2,256,256]{3,2,1,0:T(8,128)(2,1)} %get-tuple-element.643, bf16[6,1,256,256]{3,2,1,0:T(8,128)(2,1)} %get-tuple-element.770, ...), kind=kOutput, calls=%fused_computation | convolution fusion | flops 1615331328 | bytes 7340036 | tf_op jit(solution)/shard_map/while/body/eval_jaxpr/cond/branch_1_fun/bdij,cdjk->bcik/dot_general | solution.py:88
  111.7 3.1 collective-permute-done
  116.0 13.1 %conditional.4 = (f32[4,6,2,256,256]{4,3,2,1,0:T(8,128)}, f32[4,6,2,256,256]{4,3,2,1,0:T(8,128)}, bf16[6,2,256,256]{3,2,1,0:T(8,128)(2,1)}) conditional(s32[]{:T(128)} %convert_element_type.228, (f32[4,6,2,256,256]{4,3,2,1,0:T(8,128)}, f32[4,6,2,256,256]{4,3,2,1,0:T(8,128)}) %tuple.175, (pred[]{:T(512)}, bf16[6,2,256,256]{3,2,1,0:T(8,128)(2,1)}, ...), branch_computations={%region_1.1_spmd, %region_2.2_spmd} | conditional | flops 1620049920 | bytes 24642124 | solution.py:163
  116.0 4.7 %bitcast_dynamic-update-slice_fusion.1 = (f32[4,6,2,256,256]{4,3,2,1,0:T(8,128)}, f32[6,2,256,256]{3,2,1,0:T(8,128)S(1)}) fusion(f32[4,6,2,256,256]{4,3,2,1,0:T(8,128)} %get-tuple-element.636, s32[]{:T(128)S(6)} %min.20, f32[6,2,256,256]{3,2,1,0:T(8,128)} %get-tuple-element.638, bf16[6,2,256,256]{3,2,1,0:T(8,128)(2,1)} %get-tuple-element.639, ...), kind=kLoop, calls=%fused_computation.2 | loop fusion | flops 1572864 | bytes 11010564 | tf_op jit(solution)/shard_map/while/body/eval_jaxpr/cond/branch_1_fun/jit(dynamic_update_index_in_dim)/dynamic_update_slice | solution.py:156
  121.8 1.6 subtract_convert_fusion
  123.5 5.7 %bitcast_dynamic-update-slice_fusion = (f32[4,6,2,256,256]{4,3,2,1,0:T(8,128)}, bf16[6,256,2,256,1]{3,1,4,2,0:T(8,128)(2,1)}) fusion(f32[4,6,2,256,256]{4,3,2,1,0:T(8,128)} %get-tuple-element.641, s32[]{:T(128)S(6)} %min.20, bf16[2,2,256,256]{3,2,1,0:T(8,128)(2,1)} %get-tuple-element.643, bf16[6,1,256,256]{3,2,1,0:T(8,128)(2,1)} %get-tuple-element.770, ...), kind=kOutput, calls=%fused_computation | convolution fusion | flops 1615331328 | bytes 7340036 | tf_op jit(solution)/shard_map/while/body/eval_jaxpr/cond/branch_1_fun/bdij,cdjk->bcik/dot_general | solution.py:88
  130.6 3.1 collective-permute-done
  136.2 13.2 %collective-permute-start = (bf16[6,2,256,256]{3,2,1,0:T(8,128)(2,1)}, bf16[6,2,256,256]{3,2,1,0:T(8,128)(2,1)S(1)}, u32[]{:S(2)}, u32[]{:S(2)}) collective-permute-start(bf16[6,2,256,256]{3,2,1,0:T(8,128)(2,1)} %get-tuple-element.949), channel_id=1, source_target_pairs={{0,1},{2,3},{4,5},{6,7},{8,9},{10,11},{12,13},{14,15},{16,17},{18,... | collective-permute-start | bytes 4718600 | tf_op jit(solution)/shard_map/while/body/eval_jaxpr/ppermute | solution.py:25
  149.4 3.1 collective-permute-done
  153.7 6.1 %multiply_reduce_fusion = f32[4,256,256]{2,1,0:T(8,128)S(1)} fusion(f32[4,6,2,256,256]{4,3,2,1,0:T(8,128)} %get-tuple-element.686), kind=kLoop, calls=%fused_computation.35 | loop fusion | flops 6029312 | bytes 13631488 | tf_op jit(solution)/shard_map/reduce_sum | solution.py:93
  160.3 8.8 %multiply_convert_fusion = bf16[4,6,2,256,256]{4,3,2,1,0:T(8,128)(2,1)} fusion(f32[4,6,2,256,256]{4,3,2,1,0:T(8,128)} %get-tuple-element.686, f32[4,256,256]{2,1,0:T(8,128)S(1)} %subtract_multiply_fusion), kind=kLoop, calls=%fused_computation.34 | loop fusion | flops 6291456 | bytes 19922944 | tf_op jit(solution)/shard_map/convert_element_type | solution.py:96
  169.1 6.0 %broadcast_in_dim.69 = f32[4,6,2,256,256]{4,3,2,1,0:T(8,128)} broadcast(f32[]{:T(128)} %constant.277.clone.1), dimensions={} | broadcast | bytes 12582916 | tf_op jit(solution)/shard_map/broadcast_in_dim | solution.py:169
  176.4 74.6 %while.57 = (s32[]{:T(128)}, bf16[6,2,256,256]{3,2,1,0:T(8,128)(2,1)}, f32[4,6,2,256,256]{4,3,2,1,0:T(8,128)}, s32[]{:T(128)}, pred[]{:T(512)}, /*index=5*/bf16[...) while((s32[]{:T(128)}, ...), condition=%wide.region_10.11_spmd, body=%wide.region_7.10_spmd.sunk | while | flops 1616117760 | bytes 32507724 | solution.py:195
  179.0 10.2 %collective-permute-done.1 = bf16[6,2,256,256]{3,2,1,0:T(8,128)(2,1)S(1)} collective-permute-done((bf16[6,2,256,256]{3,2,1,0:T(8,128)(2,1)}, bf16[6,2,256,256]{3,2,1,0:T(8,128)(2,1)S(1)}, u32[]{:S(2)}, u32[]{:S(2)}) %collective-permute-start.1) | collective-permute-done | bytes 1572896 | tf_op jit(solution)/shard_map/while/body/eval_jaxpr/ppermute | solution.py:25
  190.3 8.5 %conditional.5 = (f32[4,6,2,256,256]{4,3,2,1,0:T(8,128)}, bf16[6,2,256,256]{3,2,1,0:T(8,128)(2,1)}) conditional(s32[]{:T(128)} %convert_element_type.229, f32[4,6,2,256,256]{4,3,2,1,0:T(8,128)} %get-tuple-element.1047, (pred[]{:T(512)}, s32[]{:T(128)}, bf16[4,6,2,256,256]{4,3,2,1,0:T(8,128)(2,1)}, bf16[6,2,256,256]{3,2,1,0:T(8,128)(2,1)}, ...), branch_computations={%region_8.8_spmd, %region_9.9_spmd} | conditional | flops 1616117760 | bytes 19924540 | solution.py:191
  190.3 5.7 %bitcast_dynamic-update-slice_fusion.2 = (f32[4,6,2,256,256]{4,3,2,1,0:T(8,128)}, f32[6,256,2,256,1]{3,1,4,2,0:T(8,128)S(1)}) fusion(f32[4,6,2,256,256]{4,3,2,1,0:T(8,128)} %get-tuple-element.657, s32[]{:T(128)S(6)} %min.21, bf16[2,2,256,256]{3,2,1,0:T(8,128)(2,1)} %get-tuple-element.662, bf16[6,2,256,256]{3,2,1,0:T(8,128)(2,1)} %get-tuple-element.661, ...), kind=kOutput, calls=%fused_computation.15 | convolution fusion | flops 1612185600 | bytes 10487296 | tf_op jit(solution)/shard_map/while/body/eval_jaxpr/cond/branch_1_fun/bdij,cdjk->bcik/dot_general | solution.py:88
  200.2 4.2 %collective-permute-done.1 = bf16[6,2,256,256]{3,2,1,0:T(8,128)(2,1)S(1)} collective-permute-done((bf16[6,2,256,256]{3,2,1,0:T(8,128)(2,1)}, bf16[6,2,256,256]{3,2,1,0:T(8,128)(2,1)S(1)}, u32[]{:S(2)}, u32[]{:S(2)}) %collective-permute-start.1) | collective-permute-done | bytes 1572896 | tf_op jit(solution)/shard_map/while/body/eval_jaxpr/ppermute | solution.py:25
  205.5 8.5 %conditional.5 = (f32[4,6,2,256,256]{4,3,2,1,0:T(8,128)}, bf16[6,2,256,256]{3,2,1,0:T(8,128)(2,1)}) conditional(s32[]{:T(128)} %convert_element_type.229, f32[4,6,2,256,256]{4,3,2,1,0:T(8,128)} %get-tuple-element.1047, (pred[]{:T(512)}, s32[]{:T(128)}, bf16[4,6,2,256,256]{4,3,2,1,0:T(8,128)(2,1)}, bf16[6,2,256,256]{3,2,1,0:T(8,128)(2,1)}, ...), branch_computations={%region_8.8_spmd, %region_9.9_spmd} | conditional | flops 1616117760 | bytes 19924540 | solution.py:191
  205.5 5.6 %bitcast_dynamic-update-slice_fusion.2 = (f32[4,6,2,256,256]{4,3,2,1,0:T(8,128)}, f32[6,256,2,256,1]{3,1,4,2,0:T(8,128)S(1)}) fusion(f32[4,6,2,256,256]{4,3,2,1,0:T(8,128)} %get-tuple-element.657, s32[]{:T(128)S(6)} %min.21, bf16[2,2,256,256]{3,2,1,0:T(8,128)(2,1)} %get-tuple-element.662, bf16[6,2,256,256]{3,2,1,0:T(8,128)(2,1)} %get-tuple-element.661, ...), kind=kOutput, calls=%fused_computation.15 | convolution fusion | flops 1612185600 | bytes 10487296 | tf_op jit(solution)/shard_map/while/body/eval_jaxpr/cond/branch_1_fun/bdij,cdjk->bcik/dot_general | solution.py:88
  215.3 4.2 %collective-permute-done.1 = bf16[6,2,256,256]{3,2,1,0:T(8,128)(2,1)S(1)} collective-permute-done((bf16[6,2,256,256]{3,2,1,0:T(8,128)(2,1)}, bf16[6,2,256,256]{3,2,1,0:T(8,128)(2,1)S(1)}, u32[]{:S(2)}, u32[]{:S(2)}) %collective-permute-start.1) | collective-permute-done | bytes 1572896 | tf_op jit(solution)/shard_map/while/body/eval_jaxpr/ppermute | solution.py:25
  220.6 8.5 %conditional.5 = (f32[4,6,2,256,256]{4,3,2,1,0:T(8,128)}, bf16[6,2,256,256]{3,2,1,0:T(8,128)(2,1)}) conditional(s32[]{:T(128)} %convert_element_type.229, f32[4,6,2,256,256]{4,3,2,1,0:T(8,128)} %get-tuple-element.1047, (pred[]{:T(512)}, s32[]{:T(128)}, bf16[4,6,2,256,256]{4,3,2,1,0:T(8,128)(2,1)}, bf16[6,2,256,256]{3,2,1,0:T(8,128)(2,1)}, ...), branch_computations={%region_8.8_spmd, %region_9.9_spmd} | conditional | flops 1616117760 | bytes 19924540 | solution.py:191
  220.6 5.7 %bitcast_dynamic-update-slice_fusion.2 = (f32[4,6,2,256,256]{4,3,2,1,0:T(8,128)}, f32[6,256,2,256,1]{3,1,4,2,0:T(8,128)S(1)}) fusion(f32[4,6,2,256,256]{4,3,2,1,0:T(8,128)} %get-tuple-element.657, s32[]{:T(128)S(6)} %min.21, bf16[2,2,256,256]{3,2,1,0:T(8,128)(2,1)} %get-tuple-element.662, bf16[6,2,256,256]{3,2,1,0:T(8,128)(2,1)} %get-tuple-element.661, ...), kind=kOutput, calls=%fused_computation.15 | convolution fusion | flops 1612185600 | bytes 10487296 | tf_op jit(solution)/shard_map/while/body/eval_jaxpr/cond/branch_1_fun/bdij,cdjk->bcik/dot_general | solution.py:88
  230.4 4.2 %collective-permute-done.1 = bf16[6,2,256,256]{3,2,1,0:T(8,128)(2,1)S(1)} collective-permute-done((bf16[6,2,256,256]{3,2,1,0:T(8,128)(2,1)}, bf16[6,2,256,256]{3,2,1,0:T(8,128)(2,1)S(1)}, u32[]{:S(2)}, u32[]{:S(2)}) %collective-permute-start.1) | collective-permute-done | bytes 1572896 | tf_op jit(solution)/shard_map/while/body/eval_jaxpr/ppermute | solution.py:25
  235.8 8.5 %conditional.5 = (f32[4,6,2,256,256]{4,3,2,1,0:T(8,128)}, bf16[6,2,256,256]{3,2,1,0:T(8,128)(2,1)}) conditional(s32[]{:T(128)} %convert_element_type.229, f32[4,6,2,256,256]{4,3,2,1,0:T(8,128)} %get-tuple-element.1047, (pred[]{:T(512)}, s32[]{:T(128)}, bf16[4,6,2,256,256]{4,3,2,1,0:T(8,128)(2,1)}, bf16[6,2,256,256]{3,2,1,0:T(8,128)(2,1)}, ...), branch_computations={%region_8.8_spmd, %region_9.9_spmd} | conditional | flops 1616117760 | bytes 19924540 | solution.py:191
  235.8 5.7 %bitcast_dynamic-update-slice_fusion.2 = (f32[4,6,2,256,256]{4,3,2,1,0:T(8,128)}, f32[6,256,2,256,1]{3,1,4,2,0:T(8,128)S(1)}) fusion(f32[4,6,2,256,256]{4,3,2,1,0:T(8,128)} %get-tuple-element.657, s32[]{:T(128)S(6)} %min.21, bf16[2,2,256,256]{3,2,1,0:T(8,128)(2,1)} %get-tuple-element.662, bf16[6,2,256,256]{3,2,1,0:T(8,128)(2,1)} %get-tuple-element.661, ...), kind=kOutput, calls=%fused_computation.15 | convolution fusion | flops 1612185600 | bytes 10487296 | tf_op jit(solution)/shard_map/while/body/eval_jaxpr/cond/branch_1_fun/bdij,cdjk->bcik/dot_general | solution.py:88
  245.6 4.2 %collective-permute-done.1 = bf16[6,2,256,256]{3,2,1,0:T(8,128)(2,1)S(1)} collective-permute-done((bf16[6,2,256,256]{3,2,1,0:T(8,128)(2,1)}, bf16[6,2,256,256]{3,2,1,0:T(8,128)(2,1)S(1)}, u32[]{:S(2)}, u32[]{:S(2)}) %collective-permute-start.1) | collective-permute-done | bytes 1572896 | tf_op jit(solution)/shard_map/while/body/eval_jaxpr/ppermute | solution.py:25
  251.0 9.2 %multiply_add_fusion = (f32[4,6,1,256,256]{4,3,2,1,0:T(8,128)S(1)}, f32[4,6,1,256,256]{4,3,2,1,0:T(8,128)S(1)}) fusion(f32[4,6,2,256,256]{4,3,2,1,0:T(8,128)} %get-tuple-element.687, f32[4,6,2,256,256]{4,3,2,1,0:T(8,128)} %get-tuple-element.685), kind=kLoop, calls=%fused_computation.37 | loop fusion | flops 9437184 | bytes 37748736 | tf_op jit(solution)/shard_map/add | solution.py:45
  260.2 2.3 maximum_reduce_fusion
  262.5 1.8 broadcast_in_dim.68
  264.4 51.8 %while.58 = (s32[]{:T(128)}, f32[2,1024,384]{2,1,0:T(8,128)}, s32[4]{0:T(128)S(1)}, s32[4]{0:T(128)S(1)}, f32[4,2,256,256]{3,2,1,0:T(8,128)}, /*index=5*/s32[]{:T(128)}, s32[]{:T(128)}, s32[]{:T(128)}, s32[]{:T(128)}) while((s32[]{:T(128)}, f32[2,1024,384]{2,1,0:T(8,128)}, s32[4]{0:T(128)S(1)}, s32[4]{0:T(128)S(1)}, ...), condition=%wide.region_13.14_spmd, body=%wide.region_12.13_spmd.sunk | while | flops 131080 | bytes 2621641 | solution.py:108
  270.9 6.5 %dynamic_update_slice.30 = f32[2,1024,384]{2,1,0:T(8,128)} dynamic-update-slice(f32[2,1024,384]{2,1,0:T(8,128)} %get-tuple-element.1077, f32[2,256,256]{2,1,0:T(8,128)S(1)} %bitcast_add_fusion.2, s32[]{:T(128)} %constant.276.clone.1..sunk.2, s32[]{:T(128)S(6)} %select_n.333, s32[]{:T(128)S(6)} %select_n.334) | dynamic-update-slice | bytes 1048580 | tf_op jit(solution)/shard_map/while/body/eval_jaxpr/dynamic_update_slice | solution.py:106
  284.1 6.5 %dynamic_update_slice.30 = f32[2,1024,384]{2,1,0:T(8,128)} dynamic-update-slice(f32[2,1024,384]{2,1,0:T(8,128)} %get-tuple-element.1077, f32[2,256,256]{2,1,0:T(8,128)S(1)} %bitcast_add_fusion.2, s32[]{:T(128)} %constant.276.clone.1..sunk.2, s32[]{:T(128)S(6)} %select_n.333, s32[]{:T(128)S(6)} %select_n.334) | dynamic-update-slice | bytes 1048580 | tf_op jit(solution)/shard_map/while/body/eval_jaxpr/dynamic_update_slice | solution.py:106
  297.1 5.9 %dynamic_update_slice.30 = f32[2,1024,384]{2,1,0:T(8,128)} dynamic-update-slice(f32[2,1024,384]{2,1,0:T(8,128)} %get-tuple-element.1077, f32[2,256,256]{2,1,0:T(8,128)S(1)} %bitcast_add_fusion.2, s32[]{:T(128)} %constant.276.clone.1..sunk.2, s32[]{:T(128)S(6)} %select_n.333, s32[]{:T(128)S(6)} %select_n.334) | dynamic-update-slice | bytes 1048580 | tf_op jit(solution)/shard_map/while/body/eval_jaxpr/dynamic_update_slice | solution.py:106
  309.7 6.5 %dynamic_update_slice.30 = f32[2,1024,384]{2,1,0:T(8,128)} dynamic-update-slice(f32[2,1024,384]{2,1,0:T(8,128)} %get-tuple-element.1077, f32[2,256,256]{2,1,0:T(8,128)S(1)} %bitcast_add_fusion.2, s32[]{:T(128)} %constant.276.clone.1..sunk.2, s32[]{:T(128)S(6)} %select_n.333, s32[]{:T(128)S(6)} %select_n.334) | dynamic-update-slice | bytes 1048580 | tf_op jit(solution)/shard_map/while/body/eval_jaxpr/dynamic_update_slice | solution.py:106
  316.2 2.1 convert.76
  318.4 1.9 collective-permute-start.4
  320.3 9.2 %collective-permute-start.5 = (bf16[2,1024,128]{2,1,0:T(8,128)(2,1)S(1)}, bf16[2,1024,128]{2,1,0:T(8,128)(2,1)S(1)}, u32[]{:S(2)}, u32[]{:S(2)}) collective-permute-start(bf16[2,1024,128]{2,1,0:T(8,128)(2,1)S(1)} %get-tuple-element.778), channel_id=1, source_target_pairs={{2,0},{4,2},{6,4},{8,6},{10,8},{12,10},{14,12},{16,14},{18,16},{20... | collective-permute-start | bytes 1572872 | tf_op jit(solution)/shard_map/ppermute | solution.py:25
  329.6 10.3 %collective-permute-done.4 = bf16[2,1024,128]{2,1,0:T(8,128)(2,1)S(1)} collective-permute-done((bf16[2,1024,128]{2,1,0:T(8,128)(2,1)S(1)}, bf16[2,1024,128]{2,1,0:T(8,128)(2,1)S(1)}, u32[]{:S(2)}, u32[]{:S(2)}) %collective-permute-start.4) | collective-permute-done | bytes 524320 | tf_op jit(solution)/shard_map/ppermute | solution.py:25
  341.0 2.3 add_bitcast_fusion
  (110 shorter events, 74.0 us)
Async XLA Ops:
  0.0 16.3 %copy-start.8 = (s32[4]{0:T(128)S(1)}, s32[4]{0:T(128)}, u32[]{:S(2)}) copy-start(s32[4]{0:T(128)} %param.30) | copy-start | bytes 52
  0.0 16.3 %copy-start.9 = (s32[4]{0:T(128)S(1)}, s32[4]{0:T(128)}, u32[]{:S(2)}) copy-start(s32[4]{0:T(128)} %param.31) | copy-start | bytes 52
  0.0 17.2 %copy-start.6 = (s32[4]{0:T(128)S(1)}, s32[4]{0:T(128)}, u32[]{:S(2)}) copy-start(s32[4]{0:T(128)} %param.33) | copy-start | bytes 52
  0.0 17.2 %copy-start.5 = (f32[16]{0:T(128)S(1)}, f32[16]{0:T(128)}, u32[]{:S(2)}) copy-start(f32[16]{0:T(128)} %param.34) | copy-start | bytes 196
  0.0 17.2 %copy-start.7 = (f32[16]{0:T(128)S(1)}, f32[16]{0:T(128)}, u32[]{:S(2)}) copy-start(f32[16]{0:T(128)} %param.35) | copy-start | bytes 196
  0.0 31.4 %collective-permute-start.2 = (f32[2,1024,128]{2,1,0:T(8,128)}, f32[2,1024,128]{2,1,0:T(8,128)S(1)}, u32[]{:S(2)}, u32[]{:S(2)}) collective-permute-start(f32[2,1024,128]{2,1,0:T(8,128)} %bitcast.162), channel_id=1, source_target_pairs={{0,2},{2,4},{4,6},{6,8},{8,10},{10,12},{12,14},{14,16},{16,18},{18... | collective-permute-start | bytes 3145736 | tf_op jit(solution)/shard_map/ppermute | solution.py:14
  3.6 29.1 %collective-permute-start.3 = (f32[2,1024,128]{2,1,0:T(8,128)}, f32[2,1024,128]{2,1,0:T(8,128)}, u32[]{:S(2)}, u32[]{:S(2)}) collective-permute-start(f32[2,1024,128]{2,1,0:T(8,128)} %bitcast.163), channel_id=1, source_target_pairs={{2,0},{4,2},{6,4},{8,6},{10,8},{12,10},{14,12},{16,14},{18,16},{20... | collective-permute-start | bytes 3145736 | tf_op jit(solution)/shard_map/ppermute | solution.py:17
  20.4 12.3 %copy-start.3 = (f32[1,2,1024,128]{3,2,1,0:T(8,128)S(1)}, f32[1,2,1024,128]{3,2,1,0:T(8,128)}, u32[]{:S(2)}) copy-start(f32[1,2,1024,128]{3,2,1,0:T(8,128)} %param.27) | copy-start | bytes 3145732
  31.4 1.0 copy-start.4
  72.7 4.5 %collective-permute-start = (bf16[6,2,256,256]{3,2,1,0:T(8,128)(2,1)}, bf16[6,2,256,256]{3,2,1,0:T(8,128)(2,1)S(1)}, u32[]{:S(2)}, u32[]{:S(2)}) collective-permute-start(bf16[6,2,256,256]{3,2,1,0:T(8,128)(2,1)} %get-tuple-element.949), channel_id=1, source_target_pairs={{0,1},{2,3},{4,5},{6,7},{8,9},{10,11},{12,13},{14,15},{16,17},{18,... | collective-permute-start | bytes 4718600 | tf_op jit(solution)/shard_map/while/body/eval_jaxpr/ppermute | solution.py:25
  77.2 1.2 copy-start
  91.5 4.5 %collective-permute-start = (bf16[6,2,256,256]{3,2,1,0:T(8,128)(2,1)}, bf16[6,2,256,256]{3,2,1,0:T(8,128)(2,1)S(1)}, u32[]{:S(2)}, u32[]{:S(2)}) collective-permute-start(bf16[6,2,256,256]{3,2,1,0:T(8,128)(2,1)} %get-tuple-element.949), channel_id=1, source_target_pairs={{0,1},{2,3},{4,5},{6,7},{8,9},{10,11},{12,13},{14,15},{16,17},{18,... | collective-permute-start | bytes 4718600 | tf_op jit(solution)/shard_map/while/body/eval_jaxpr/ppermute | solution.py:25
  96.0 1.2 copy-start
  110.3 4.5 %collective-permute-start = (bf16[6,2,256,256]{3,2,1,0:T(8,128)(2,1)}, bf16[6,2,256,256]{3,2,1,0:T(8,128)(2,1)S(1)}, u32[]{:S(2)}, u32[]{:S(2)}) collective-permute-start(bf16[6,2,256,256]{3,2,1,0:T(8,128)(2,1)} %get-tuple-element.949), channel_id=1, source_target_pairs={{0,1},{2,3},{4,5},{6,7},{8,9},{10,11},{12,13},{14,15},{16,17},{18,... | collective-permute-start | bytes 4718600 | tf_op jit(solution)/shard_map/while/body/eval_jaxpr/ppermute | solution.py:25
  114.8 1.2 copy-start
  129.1 4.5 %collective-permute-start = (bf16[6,2,256,256]{3,2,1,0:T(8,128)(2,1)}, bf16[6,2,256,256]{3,2,1,0:T(8,128)(2,1)S(1)}, u32[]{:S(2)}, u32[]{:S(2)}) collective-permute-start(bf16[6,2,256,256]{3,2,1,0:T(8,128)(2,1)} %get-tuple-element.949), channel_id=1, source_target_pairs={{0,1},{2,3},{4,5},{6,7},{8,9},{10,11},{12,13},{14,15},{16,17},{18,... | collective-permute-start | bytes 4718600 | tf_op jit(solution)/shard_map/while/body/eval_jaxpr/ppermute | solution.py:25
  133.7 1.2 copy-start
  136.2 16.4 %collective-permute-start = (bf16[6,2,256,256]{3,2,1,0:T(8,128)(2,1)}, bf16[6,2,256,256]{3,2,1,0:T(8,128)(2,1)S(1)}, u32[]{:S(2)}, u32[]{:S(2)}) collective-permute-start(bf16[6,2,256,256]{3,2,1,0:T(8,128)(2,1)} %get-tuple-element.949), channel_id=1, source_target_pairs={{0,1},{2,3},{4,5},{6,7},{8,9},{10,11},{12,13},{14,15},{16,17},{18,... | collective-permute-start | bytes 4718600 | tf_op jit(solution)/shard_map/while/body/eval_jaxpr/ppermute | solution.py:25
  152.5 1.2 copy-start
  153.7 6.1 %copy-start.2 = (f32[4,256,256]{2,1,0:T(8,128)S(1)}, f32[4,256,256]{2,1,0:T(8,128)}, u32[]{:S(2)}) copy-start(f32[4,256,256]{2,1,0:T(8,128)} %param.29) | copy-start | bytes 3145732
  177.7 11.5 %collective-permute-start.1 = (bf16[6,2,256,256]{3,2,1,0:T(8,128)(2,1)}, bf16[6,2,256,256]{3,2,1,0:T(8,128)(2,1)S(1)}, u32[]{:S(2)}, u32[]{:S(2)}) collective-permute-start(bf16[6,2,256,256]{3,2,1,0:T(8,128)(2,1)} %get-tuple-element.960), channel_id=1, source_target_pairs={{1,0},{3,2},{5,4},{7,6},{9,8},{11,10},{13,12},{15,14},{17,16},{19,... | collective-permute-start | bytes 4718600 | tf_op jit(solution)/shard_map/while/body/eval_jaxpr/ppermute | solution.py:25
  189.2 1.2 copy-start.1
  198.9 5.5 %collective-permute-start.1 = (bf16[6,2,256,256]{3,2,1,0:T(8,128)(2,1)}, bf16[6,2,256,256]{3,2,1,0:T(8,128)(2,1)S(1)}, u32[]{:S(2)}, u32[]{:S(2)}) collective-permute-start(bf16[6,2,256,256]{3,2,1,0:T(8,128)(2,1)} %get-tuple-element.960), channel_id=1, source_target_pairs={{1,0},{3,2},{5,4},{7,6},{9,8},{11,10},{13,12},{15,14},{17,16},{19,... | collective-permute-start | bytes 4718600 | tf_op jit(solution)/shard_map/while/body/eval_jaxpr/ppermute | solution.py:25
  204.4 1.2 copy-start.1
  214.0 5.5 %collective-permute-start.1 = (bf16[6,2,256,256]{3,2,1,0:T(8,128)(2,1)}, bf16[6,2,256,256]{3,2,1,0:T(8,128)(2,1)S(1)}, u32[]{:S(2)}, u32[]{:S(2)}) collective-permute-start(bf16[6,2,256,256]{3,2,1,0:T(8,128)(2,1)} %get-tuple-element.960), channel_id=1, source_target_pairs={{1,0},{3,2},{5,4},{7,6},{9,8},{11,10},{13,12},{15,14},{17,16},{19,... | collective-permute-start | bytes 4718600 | tf_op jit(solution)/shard_map/while/body/eval_jaxpr/ppermute | solution.py:25
  219.5 1.2 copy-start.1
  229.1 5.5 %collective-permute-start.1 = (bf16[6,2,256,256]{3,2,1,0:T(8,128)(2,1)}, bf16[6,2,256,256]{3,2,1,0:T(8,128)(2,1)S(1)}, u32[]{:S(2)}, u32[]{:S(2)}) collective-permute-start(bf16[6,2,256,256]{3,2,1,0:T(8,128)(2,1)} %get-tuple-element.960), channel_id=1, source_target_pairs={{1,0},{3,2},{5,4},{7,6},{9,8},{11,10},{13,12},{15,14},{17,16},{19,... | collective-permute-start | bytes 4718600 | tf_op jit(solution)/shard_map/while/body/eval_jaxpr/ppermute | solution.py:25
  234.6 1.2 copy-start.1
  244.3 5.5 %collective-permute-start.1 = (bf16[6,2,256,256]{3,2,1,0:T(8,128)(2,1)}, bf16[6,2,256,256]{3,2,1,0:T(8,128)(2,1)S(1)}, u32[]{:S(2)}, u32[]{:S(2)}) collective-permute-start(bf16[6,2,256,256]{3,2,1,0:T(8,128)(2,1)} %get-tuple-element.960), channel_id=1, source_target_pairs={{1,0},{3,2},{5,4},{7,6},{9,8},{11,10},{13,12},{15,14},{17,16},{19,... | collective-permute-start | bytes 4718600 | tf_op jit(solution)/shard_map/while/body/eval_jaxpr/ppermute | solution.py:25
  249.8 1.2 copy-start.1
  318.4 21.4 %collective-permute-start.4 = (bf16[2,1024,128]{2,1,0:T(8,128)(2,1)S(1)}, bf16[2,1024,128]{2,1,0:T(8,128)(2,1)S(1)}, u32[]{:S(2)}, u32[]{:S(2)}) collective-permute-start(bf16[2,1024,128]{2,1,0:T(8,128)(2,1)S(1)} %get-tuple-element.777), channel_id=1, source_target_pairs={{0,2},{2,4},{4,6},{6,8},{8,10},{10,12},{12,14},{14,16},{16,18},{18... | collective-permute-start | bytes 1572872 | tf_op jit(solution)/shard_map/ppermute | solution.py:25
  320.3 20.7 %collective-permute-start.5 = (bf16[2,1024,128]{2,1,0:T(8,128)(2,1)S(1)}, bf16[2,1024,128]{2,1,0:T(8,128)(2,1)S(1)}, u32[]{:S(2)}, u32[]{:S(2)}) collective-permute-start(bf16[2,1024,128]{2,1,0:T(8,128)(2,1)S(1)} %get-tuple-element.778), channel_id=1, source_target_pairs={{2,0},{4,2},{6,4},{8,6},{10,8},{12,10},{14,12},{16,14},{18,16},{20... | collective-permute-start | bytes 1572872 | tf_op jit(solution)/shard_map/ppermute | solution.py:25
where the time goes:
time: 347 us; the launch traced here: 343 us
  local copies, waits for them, and re-layouts  88.5 us (26%)
  other arithmetic  76.1 us (22%)
  waiting for transfers between devices  64.1 us (18%)
  matrix products  51.2 us (15%)
  starting transfers between devices  46.6 us (13%)
  loops' own time  16 us (5%)
    ppermute x12, waiting for transfers between devices, shifted(): return lax.ppermute(block, axis, route)  54.1 us
    dot_general x8, matrix products, apply_sides(): jnp.einsum('bdij,cdjk->bcik', inner, table, preferred_element_type=jnp.fl...  45.2 us
    ppermute x12, starting transfers between devices, shifted(): return lax.ppermute(block, axis, route)  36.4 us
    dynamic_update_slice x4, local copies, waits for them, and re-layouts, add_one(): lax.dynamic_update_slice(current, present + contributions[position], place)  25.5 us
    dynamic_update_slice x4, other arithmetic, forward_compute(): lax.dynamic_update_index_in_dim(saved_pair[0], wave_in, chosen, 0)  18.9 us
    broadcast_in_dim x3, local copies, waits for them, and re-layouts, shards(): stored = jnp.zeros((slot_count,) + wave_shape, jnp.float32)  18.1 us
    another operation x1, loops' own time, add_patches(): return lax.fori_loop(0, contributions.shape[0], add_one, gradient)  15.6 us
    another operation x12, other arithmetic  13.4 us
  transfers between devices with their start and end apart: 14, of which 14 were waited for; matrix products, arithmetic and copies ran while one was open for 3% of the time, Pallas kernels for 0%

commit v1 on v0

v1 whole, which is shorter than its diff:
```python
import functools
import math

import jax
import jax.numpy as jnp
import numpy as np
from jax import lax
from jax.experimental import pallas as pl
from jax.experimental.pallas import tpu as pltpu
from jax.sharding import PartitionSpec as P

L = 256
Q = 128
MODES = 6
GROUP = 3
SLOTS = 2
ROWS = 1024
BF = jnp.bfloat16
F32 = jnp.float32
VMEM = pltpu.VMEM
SMEM = pltpu.SMEM


def rounded(values):
    return np.asarray(values, np.float32).astype(jnp.bfloat16).astype(np.float64)


def block(values):
    re, im = values.real, values.imag
    full = np.block([[re, -im], [im, re]])
    return np.stack([full, full.T])


@functools.cache
def tables():
    k = np.arange(L)
    dft = np.exp(-2j * np.pi / L * (k[:, None] * k[None, :] % L)) / math.sqrt(L)
    signed = np.where(k < Q, k, k - L)
    filt = np.exp(-1j * np.pi / L * (signed * signed % (2 * L)))
    prop = dft.conj() @ (filt[:, None] * dft)
    prop = rounded(prop.real) + 1j * rounded(prop.imag)
    dft = rounded(dft.real) + 1j * rounded(dft.imag)
    near, far = prop[:Q, :Q], prop[:Q, Q:]
    halves = [(near + far) / 2, (near - far) / 2]
    kinds = [[block(h) for h in halves], [block(dft[0::2, :Q]), block(dft[1::2, :Q])]]
    return np.stack([np.stack(kind) for kind in kinds]).astype(np.float32)


@functools.cache
def lane_split():
    k = np.arange(L)
    return (k[:, None] == np.where(k < Q, 2 * k, 2 * (k - Q) + 1)[None, :]).astype(np.float32)


def dot(a, b):
    return jnp.dot(a, b, preferred_element_type=F32)


def hadamard(q):
    s0, d0 = q[0][0] + q[0][1], q[0][0] - q[0][1]
    s1, d1 = q[1][0] + q[1][1], q[1][0] - q[1][1]
    return [[s0 + s1, d0 + d1], [s0 - s1, d0 - d1]]


def quads(fn):
    return [[fn(i, j) for j in range(2)] for i in range(2)]


CH = 16


def store_waves(z_ref, m, r, re, im):
    for i in range(2):
        for j in range(2):
            z_ref[m, i, r : r + CH, Q * j : Q * j + Q] = re[i][j].astype(BF)
            z_ref[m, i, Q + r : Q + r + CH, Q * j : Q * j + Q] = im[i][j].astype(BF)


def left_side(table, kind, back, z_ref, u_ref, m):
    for i in range(2):
        u = dot(table[kind, i, back], z_ref[m, i]).astype(BF)
        for j in range(2):
            u_ref[m, j, Q * i : Q * i + Q, 0:Q] = u[0:Q, Q * j : Q * j + Q]
            u_ref[m, j, Q * i : Q * i + Q, Q:L] = u[Q:L, Q * j : Q * j + Q]


def right_side(table, kind, back, u_ref, w_ref, m):
    for j in range(2):
        w_ref[m, j] = dot(u_ref[m, j], table[kind, j, 1 - back])


def read_waves(w_ref, m, r):
    re = quads(lambda i, j: w_ref[m, j, Q * i + r : Q * i + r + CH, 0:Q])
    im = quads(lambda i, j: w_ref[m, j, Q * i + r : Q * i + r + CH, Q:L])
    return re, im


def rotate_probe(probe, pr_ref, col):
    lane = lax.broadcasted_iota(jnp.int32, (32, Q), 1)
    wrapped = lane < col

    def one(m, _):
        for c in range(2):
            for r in range(0, L, 32):
                a = pltpu.roll(probe[m, c, r : r + 32, 0:Q], col, 1)
                b = pltpu.roll(probe[m, c, r : r + 32, Q:L], col, 1)
                pr_ref[m, c, r : r + 32, 0:Q] = jnp.where(wrapped, b, a)
                pr_ref[m, c, r : r + 32, Q:L] = jnp.where(wrapped, a, b)
        return 0

    lax.fori_loop(0, MODES, one, 0)


def load_patch(own, left, right, o_ref, tmp, place, row, col):
    lane = lax.broadcasted_iota(jnp.int32, (CH, Q), 1)
    base = pl.multiple_of(jnp.minimum(row // 16, (ROWS - L) // 16 - 1) * 16, 16)
    off = row - base
    for c in range(2):
        for r in range(0, L + 16, 16):
            a = left[c, pl.ds(base + r, 16), :].astype(F32)
            b = right[c, pl.ds(base + r, 16), :].astype(F32)
            tmp[c, r : r + 16, :] = jnp.where(lane < col, b, a)
        o_ref[place, c, :, Q:L] = own[c, pl.ds(row, L), :]
        o_ref[place, c, :, 0:Q] = tmp[c, pl.ds(off, L), :]


def amplitudes(measured, slot, split, amp_ref, tmp_ref):
    for j in range(2):
        tmp_ref[j] = jnp.sqrt(measured[slot, :, Q * j : Q * j + Q])
    for i in range(2):
        x = jnp.concatenate([tmp_ref[j, pl.ds(i, Q, stride=2), :] for j in range(2)], axis=1)
        hi = x.astype(BF)
        rest = x - hi.astype(F32)
        mid = rest.astype(BF)
        lo = (rest - mid.astype(F32)).astype(BF)
        amp_ref[i] = dot(hi, split[...]) + (dot(mid, split[...]) + dot(lo, split[...]))


def waves_forward(table, pr_ref, o_ref, p, z, u, w, psi_ref, far_ref, int_ref):
    int_ref[...] = jnp.zeros_like(int_ref)

    def group(g, _):
        for k in range(GROUP):
            m = g * GROUP + k
            for r in range(0, Q, CH):
                re, im = [[None] * 2 for _ in range(2)], [[None] * 2 for _ in range(2)]
                for i in range(2):
                    for j in range(2):
                        rows, lanes = slice(Q * i + r, Q * i + r + CH), slice(Q * j, Q * j + Q)
                        a, b = pr_ref[m, 0, rows, lanes], pr_ref[m, 1, rows, lanes]
                        c, d = o_ref[2 * p, 0, rows, lanes], o_ref[2 * p, 1, rows, lanes]
                        re[i][j], im[i][j] = a * c - b * d, a * d + b * c
                store_waves(z, k, r, hadamard(re), hadamard(im))
        for k in range(GROUP):
            left_side(table, 0, 0, z, u, k)
        for k in range(GROUP):
            right_side(table, 0, 0, u, w, k)
        for k in range(GROUP):
            m = g * GROUP + k
            for r in range(0, Q, CH):
                vre, vim = read_waves(w, k, r)
                vre, vim = hadamard(vre), hadamard(vim)
                re, im = [[None] * 2 for _ in range(2)], [[None] * 2 for _ in range(2)]
                for i in range(2):
                    for j in range(2):
                        rows, lanes = slice(Q * i + r, Q * i + r + CH), slice(Q * j, Q * j + Q)
                        a, b = vre[i][j], vim[i][j]
                        psi_ref[m, 0, rows, lanes] = a.astype(BF)
                        psi_ref[m, 1, rows, lanes] = b.astype(BF)
                        c, d = o_ref[2 * p + 1, 0, rows, lanes], o_ref[2 * p + 1, 1, rows, lanes]
                        re[i][j], im[i][j] = a * c - b * d, a * d + b * c
                store_waves(z, k, r, hadamard(re), hadamard(im))
        for k in range(GROUP):
            left_side(table, 1, 0, z, u, k)
        for k in range(GROUP):
            for j in range(2):
                far_ref[g * GROUP + k, j] = dot(u[k, j], table[1, j, 1])
        for j in range(2):
            for r in range(0, L, CH):
                total = int_ref[j, r : r + CH, :]
                for k in range(GROUP):
                    x = far_ref[g * GROUP + k, j, r : r + CH, 0:Q]
                    y = far_ref[g * GROUP + k, j, r : r + CH, Q:L]
                    total = total + (x * x + y * y)
                int_ref[j, r : r + CH, :] = total
        return 0

    lax.fori_loop(0, MODES // GROUP, group, 0)


def residual_factor(int_ref, amp_ref, fac_ref, scale, offset, valid):
    for j in range(2):
        for i in range(2):
            intensity = scale * int_ref[j, Q * i : Q * i + Q, :] + offset
            ratio = amp_ref[i, :, Q * j : Q * j + Q] / jnp.sqrt(intensity)
            fac_ref[j, Q * i : Q * i + Q, :] = jnp.where(valid, scale * (1.0 - ratio), 0.0)


def waves_backward(table, pr_ref, o_ref, p, z, u, w, psi_ref, far_ref, fac_ref, grad_ref):
    grad_ref[pl.ds(2 * p, 2)] = jnp.zeros((2, 2, L, L), F32)

    def conj_terms(place, r, terms):
        for i in range(2):
            for j in range(2):
                rows, lanes = slice(Q * i + r, Q * i + r + CH), slice(Q * j, Q * j + Q)
                gre, gim = grad_ref[place, 0, rows, lanes], grad_ref[place, 1, rows, lanes]
                for a, b, x, y in terms(i, j, rows, lanes):
                    gre = gre + (a * x + b * y)
                    gim = gim + (a * y - b * x)
                grad_ref[place, 0, rows, lanes] = gre
                grad_ref[place, 1, rows, lanes] = gim

    def group(g, _):
        for k in range(GROUP):
            m = g * GROUP + k
            for j in range(2):
                for r in range(0, L, CH):
                    f = fac_ref[j, r : r + CH, :]
                    i, s = r // Q, r % Q
                    z[k, i, s : s + CH, Q * j : Q * j + Q] = (f * far_ref[m, j, r : r + CH, 0:Q]).astype(BF)
                    z[k, i, Q + s : Q + s + CH, Q * j : Q * j + Q] = (
                        f * far_ref[m, j, r : r + CH, Q:L]
                    ).astype(BF)
        for k in range(GROUP):
            left_side(table, 1, 1, z, u, k)
        for k in range(GROUP):
            right_side(table, 1, 1, u, w, k)
        for k in range(GROUP):
            m = g * GROUP + k
            for r in range(0, Q, CH):
                vre, vim = read_waves(w, k, r)
                vre, vim = hadamard(vre), hadamard(vim)
                conj_terms(
                    2 * p + 1,
                    r,
                    lambda i, j, rows, lanes: [
                        (
                            psi_ref[m, 0, rows, lanes].astype(F32),
                            psi_ref[m, 1, rows, lanes].astype(F32),
                            vre[i][j],
                            vim[i][j],
                        )
                    ],
                )
                re, im = [[None] * 2 for _ in range(2)], [[None] * 2 for _ in range(2)]
                for i in range(2):
                    for j in range(2):
                        rows, lanes = slice(Q * i + r, Q * i + r + CH), slice(Q * j, Q * j + Q)
                        c, d = o_ref[2 * p + 1, 0, rows, lanes], o_ref[2 * p + 1, 1, rows, lanes]
                        x, y = vre[i][j], vim[i][j]
                        re[i][j], im[i][j] = c * x + d * y, c * y - d * x
                store_waves(z, k, r, hadamard(re), hadamard(im))
        for k in range(GROUP):
            left_side(table, 0, 1, z, u, k)
        for k in range(GROUP):
            right_side(table, 0, 1, u, w, k)
        for k in range(GROUP):
            m = g * GROUP + k
            for r in range(0, Q, CH):
                vre, vim = read_waves(w, k, r)
                vre, vim = hadamard(vre), hadamard(vim)
                conj_terms(
                    2 * p,
                    r,
                    lambda i, j, rows, lanes: [
                        (pr_ref[m, 0, rows, lanes], pr_ref[m, 1, rows, lanes], vre[i][j], vim[i][j])
                    ],
                )
        return 0

    lax.fori_loop(0, MODES // GROUP, group, 0)


def wave_kernel(
    rows, cols, counts, dataset, dose, ground,
    own0, left0, right0, own1, left1, right1, probe, measured, table, split,
    own_mine, own_theirs, halo_mine, halo_theirs,
    o_ref, pr_ref, psi_ref, far_ref, int_ref, fac_ref, amp_ref, z, u, w, grad_ref, tmp,
):
    depth = lax.axis_index("depth")

    def position(p, _):
        slot = depth * SLOTS + p
        row = jnp.clip(rows[slot], 0, ROWS - L)
        col = jnp.clip(cols[slot], 0, Q - 1)
        which = jnp.clip(dataset[slot], 0, dose.shape[0] - 1)
        load_patch(own0, left0, right0, o_ref, tmp, 2 * p + depth, row, col)
        load_patch(own1, left1, right1, o_ref, tmp, 2 * p + 1 - depth, row, col)
        rotate_probe(probe, pr_ref, col)
        amplitudes(measured, slot, split, amp_ref, int_ref)
        waves_forward(table, pr_ref, o_ref, p, z, u, w, psi_ref, far_ref, int_ref)
        residual_factor(int_ref, amp_ref, fac_ref, dose[which], ground[which], slot < counts[0])
        waves_backward(table, pr_ref, o_ref, p, z, u, w, psi_ref, far_ref, fac_ref, grad_ref)
        mine, theirs = 2 * p + depth, 2 * p + 1 - depth
        own_mine[p] = grad_ref[mine, :, :, Q:L]
        own_theirs[p] = grad_ref[theirs, :, :, Q:L].astype(BF)
        halo_mine[p] = grad_ref[mine, :, :, 0:Q].astype(BF)
        halo_theirs[p] = grad_ref[theirs, :, :, 0:Q].astype(BF)
        return 0

    lax.fori_loop(0, SLOTS, position, 0)


def waves(scalars, transmissions, probe, measured):
    part = jax.ShapeDtypeStruct((SLOTS, 2, L, Q), F32)
    short = jax.ShapeDtypeStruct((SLOTS, 2, L, Q), BF)
    vm = pl.BlockSpec(memory_space=VMEM)
    return pl.pallas_call(
        wave_kernel,
        out_shape=(part, short, short, short),
        in_specs=[pl.BlockSpec(memory_space=SMEM)] * 6 + [vm] * 10,
        out_specs=(vm,) * 4,
        scratch_shapes=[
            VMEM((4, 2, L, L), F32),
            VMEM((MODES, 2, L, L), F32),
            VMEM((MODES, 2, L, L), BF),
            VMEM((MODES, 2, L, L), F32),
            VMEM((2, L, Q), F32),
            VMEM((2, L, Q), F32),
            VMEM((2, Q, L), F32),
            VMEM((GROUP, 2, L, L), BF),
            VMEM((GROUP, 2, L, L), BF),
            VMEM((GROUP, 2, L, L), F32),
            VMEM((4, 2, L, L), F32),
            VMEM((2, L + 16, Q), F32),
        ],
        compiler_params=pltpu.CompilerParams(vmem_limit_bytes=60 * 2**20),
        name="waves",
    )(
        *scalars,
        *transmissions,
        probe,
        measured,
        jnp.asarray(tables()).astype(BF),
        jnp.asarray(lane_split()).astype(BF),
    )


def combine_kernel(
    rows, lrows, lcols, rrows, rcols, mine, theirs, ll0, ll1, rr0, rr1, out
):
    depth = lax.axis_index("depth")
    lane = lax.broadcasted_iota(jnp.int32, (L, Q), 1)
    out[...] = jnp.zeros_like(out)

    def add(row, values):
        row = jnp.clip(row, 0, ROWS - L)
        for c in range(2):
            out[c, pl.ds(row, L), :] += values(c)

    for p in range(SLOTS):
        add(rows[depth * SLOTS + p], lambda c: mine[p, c])
        add(rows[(1 - depth) * SLOTS + p], lambda c: theirs[p, c].astype(F32))
        for ref, core in ((ll0, depth), (ll1, 1 - depth)):
            slot = core * SLOTS + p
            add(lrows[slot], lambda c: jnp.where(lane < lcols[slot], ref[p, c].astype(F32), 0.0))
        for ref, core in ((rr0, depth), (rr1, 1 - depth)):
            slot = core * SLOTS + p
            add(rrows[slot], lambda c: jnp.where(lane < rcols[slot], 0.0, ref[p, c].astype(F32)))


def combine(scalars, parts):
    vm = pl.BlockSpec(memory_space=VMEM)
    return pl.pallas_call(
        combine_kernel,
        out_shape=jax.ShapeDtypeStruct((2, ROWS, Q), F32),
        in_specs=[pl.BlockSpec(memory_space=SMEM)] * 5 + [vm] * 6,
        out_specs=vm,
        compiler_params=pltpu.CompilerParams(vmem_limit_bytes=60 * 2**20),
        name="combine",
    )(*scalars, *parts)


def shards(transmission, probe_modes, measured, scan_rows, scan_cols, counts, dataset, dose_scale, background):
    tiles = lax.axis_size("tile")
    up = [(i, i + 1) for i in range(tiles - 1)]
    down = [(i + 1, i) for i in range(tiles - 1)]
    swap = [(0, 1), (1, 0)]
    up_cross = [(2 * i + c, 2 * (i + 1) + 1 - c) for i in range(tiles - 1) for c in range(2)]
    down_cross = [(2 * (i + 1) + c, 2 * i + 1 - c) for i in range(tiles - 1) for c in range(2)]
    own = transmission[0, :, :, :]
    short = own.astype(BF)
    left = lax.ppermute(short, "tile", up)
    right = lax.ppermute(short, "tile", down)
    own1 = lax.ppermute(own, "depth", swap)
    left1 = lax.ppermute(left, "depth", swap)
    right1 = lax.ppermute(right, "depth", swap)
    places = jnp.stack([scan_rows, scan_cols])
    lplaces = lax.ppermute(places, "tile", up)
    rplaces = lax.ppermute(places, "tile", down)
    own_mine, own_theirs, halo_mine, halo_theirs = waves(
        (scan_rows, scan_cols, counts, dataset, dose_scale, background),
        (own, left, right, own1, left1, right1),
        probe_modes,
        measured,
    )
    theirs = lax.ppermute(own_theirs, "depth", swap)
    ll0 = lax.ppermute(halo_mine, "tile", up)
    rr0 = lax.ppermute(halo_mine, "tile", down)
    ll1 = lax.ppermute(halo_theirs, ("tile", "depth"), up_cross)
    rr1 = lax.ppermute(halo_theirs, ("tile", "depth"), down_cross)
    out = combine(
        (scan_rows, lplaces[0], lplaces[1], rplaces[0], rplaces[1]),
        (own_mine, theirs, ll0, ll1, rr0, rr1),
    )
    return out[None]


def solution(mesh):
    in_specs = (
        P("depth", None, None, "tile"),
        P(),
        P("tile", None, None),
        P("tile"),
        P("tile"),
        P("tile"),
        P("tile"),
        P(),
        P(),
    )
    out_specs = P("depth", None, None, "tile")
    return jax.shard_map(shards, mesh=mesh, in_specs=in_specs, out_specs=out_specs, check_vma=False)
```

time: 347 us -> 96.6 us (0.28)
  local copies, waits for them, and re-layouts: 88.5 us -> 3.84 us
  other arithmetic: 76.1 us -> 2.02 us
  matrix products: 51.2 us -> 0 us
  waiting for transfers between devices: 64.1 us -> 20 us
  Pallas kernels: 0 us -> 27.3 us
  loops' own time: 16 us -> 0 us
  starting transfers between devices: 46.6 us -> 41 us
    dot_general x12 -> x0, matrix products: 51.2 us -> none  [the longest x8 45.2 us: apply_sides(): jnp.einsum('bdij,cdjk->bcik', inner, table, preferred_element_type=jnp.fl...]
    ppermute x14 -> x12, waiting for transfers between devices: 64.1 us -> 20 us  [the longest x1 9.6 us: shards(): left = lax.ppermute(short, 'tile', up)]
    pallas_call x0 -> x2, Pallas kernels: none -> 27.3 us  [the longest x1 24.4 us: waves(): pl.pallas_call(wave_kernel, out_shape=(part, short, short, short), in_spe...]
    dynamic_update_slice x4 -> x0, local copies, waits for them, and re-layouts: 25.5 us -> none  [add_one(): lax.dynamic_update_slice(current, present + contributions[position], place)]
    broadcast_in_dim x4 -> x0, local copies, waits for them, and re-layouts: 20 us -> none  [the longest x3 18.1 us: shards(): stored = jnp.zeros((slot_count,) + wave_shape, jnp.float32)]
    dynamic_update_slice x4 -> x0, other arithmetic: 18.9 us -> none  [forward_compute(): lax.dynamic_update_index_in_dim(saved_pair[0], wave_in, chosen, 0)]
    another operation x18 -> x1, other arithmetic: 18.7 us -> 0.73 us  [shards(): places = jnp.stack([scan_rows, scan_cols])]
    another operation x14 -> x0, loops' own time: 16 us -> none  [the longest x1 15.6 us: add_patches(): return lax.fori_loop(0, contributions.shape[0], add_one, gradient)]
  transfers between devices with their start and end apart: 14 -> 12, of which waited for: 14 -> 4; matrix products, arithmetic and copies ran while one was open for 3% -> 2% of each run, Pallas kernels for 0% -> 26%
where the time goes in v1:
time: 96.6 us; the launch traced here: 94.9 us
  starting transfers between devices  41 us (42%)
  Pallas kernels  27.3 us (28%)
  waiting for transfers between devices  20 us (21%)
  local copies, waits for them, and re-layouts  3.84 us (4%)
  other arithmetic  2.02 us (2%)
    pallas_call x1, Pallas kernels, waves(): pl.pallas_call(wave_kernel, out_shape=(part, short, short, short), in_spe...  24.4 us
    ppermute x1, waiting for transfers between devices, shards(): left = lax.ppermute(short, 'tile', up)  9.6 us
    ppermute x1, starting transfers between devices, shards(): rplaces = lax.ppermute(places, 'tile', down)  8.6 us
    ppermute x1, starting transfers between devices, shards(): rr0 = lax.ppermute(halo_mine, 'tile', down)  8.13 us
    ppermute x1, starting transfers between devices, shards(): rr1 = lax.ppermute(halo_theirs, ('tile', 'depth'), down_cross)  7.08 us
    ppermute x1, waiting for transfers between devices, shards(): ll1 = lax.ppermute(halo_theirs, ('tile', 'depth'), up_cross)  7.07 us
    ppermute x1, starting transfers between devices, shards(): right = lax.ppermute(short, 'tile', down)  6.66 us
    ppermute x1, starting transfers between devices, shards(): left = lax.ppermute(short, 'tile', up)  3.4 us
  transfers between devices with their start and end apart: 12, of which 4 were waited for; matrix products, arithmetic and copies ran while one was open for 2% of the time, Pallas kernels for 26%

profile of v1, /device:TPU:96, one launch (start us, length us, event | category | flops | bytes accessed | tf_op | source)
XLA Modules:
  0.0 94.9 jit_solution(4823450384547948554)
XLA Ops:
  0.0 1.3 %bitcast_convert_fusion = bf16[2,1024,128]{2,1,0:T(8,128)(2,1)S(1)} fusion(f32[1,2,1024,128]{3,2,1,0:T(8,128)} %param.11), kind=kLoop, calls=%fused_computation.5 | loop fusion | flops 262144 | bytes 1572864 | tf_op jit(solution)/shard_map/convert_element_type | solution.py:382
  1.3 3.4 %collective-permute-start.2 = (bf16[2,1024,128]{2,1,0:T(8,128)(2,1)S(1)}, bf16[2,1024,128]{2,1,0:T(8,128)(2,1)S(1)}, u32[]{:S(2)}, u32[]{:S(2)}) collective-permute-start(bf16[2,1024,128]{2,1,0:T(8,128)(2,1)S(1)} %bitcast_convert_fusion), channel_id=1, source_target_pairs={{0,2},{2,4},{4,6},{6,8},{8,10},{10,12},{12,14},{14,16},{16,18},{18... | collective-permute-start | bytes 1572872 | tf_op jit(solution)/shard_map/ppermute | solution.py:383
  4.7 6.7 %collective-permute-start.3 = (bf16[2,1024,128]{2,1,0:T(8,128)(2,1)S(1)}, bf16[2,1024,128]{2,1,0:T(8,128)(2,1)S(1)}, u32[]{:S(2)}, u32[]{:S(2)}) collective-permute-start(bf16[2,1024,128]{2,1,0:T(8,128)(2,1)S(1)} %bitcast_convert_fusion), channel_id=1, source_target_pairs={{2,0},{4,2},{6,4},{8,6},{10,8},{12,10},{14,12},{16,14},{18,16},{20... | collective-permute-start | bytes 1572872 | tf_op jit(solution)/shard_map/ppermute | solution.py:384
  11.4 0.1 collective-permute-start.4
  11.5 9.6 %collective-permute-done.2.left0 = bf16[2,1024,128]{2,1,0:T(8,128)(2,1)S(1)} collective-permute-done((bf16[2,1024,128]{2,1,0:T(8,128)(2,1)S(1)}, bf16[2,1024,128]{2,1,0:T(8,128)(2,1)S(1)}, u32[]{:S(2)}, u32[]{:S(2)}) %collective-permute-start.2) | collective-permute-done | bytes 524320 | tf_op jit(solution)/shard_map/ppermute | solution.py:383
  21.1 0.0 copy-start.1
  21.1 0.0 collective-permute-start.5
  21.1 1.2 %collective-permute-done.3.right0 = bf16[2,1024,128]{2,1,0:T(8,128)(2,1)S(1)} collective-permute-done((bf16[2,1024,128]{2,1,0:T(8,128)(2,1)S(1)}, bf16[2,1024,128]{2,1,0:T(8,128)(2,1)S(1)}, u32[]{:S(2)}, u32[]{:S(2)}) %collective-permute-start.3) | collective-permute-done | bytes 524320 | tf_op jit(solution)/shard_map/ppermute | solution.py:384
  22.3 0.0 copy-start.2
  22.3 0.0 collective-permute-start.6
  22.3 0.7 pad_add_fusion
  23.0 8.6 %collective-permute-start.1 = (s32[2,4]{1,0:T(2,128)S(1)}, s32[2,4]{1,0:T(2,128)S(1)}, u32[]{:S(2)}, u32[]{:S(2)}) collective-permute-start(s32[2,4]{1,0:T(2,128)S(1)} %pad_add_fusion), channel_id=1, source_target_pairs={{2,0},{4,2},{6,4},{8,6},{10,8},{12,10},{14,12},{16,14},{18,16},{20... | collective-permute-start | bytes 104 | tf_op jit(solution)/shard_map/ppermute | solution.py:390
  31.6 1.9 %collective-permute-start = (s32[2,4]{1,0:T(2,128)S(1)}, s32[2,4]{1,0:T(2,128)S(1)}, u32[]{:S(2)}, u32[]{:S(2)}) collective-permute-start(s32[2,4]{1,0:T(2,128)S(1)} %pad_add_fusion), channel_id=1, source_target_pairs={{0,2},{2,4},{4,6},{6,8},{8,10},{10,12},{12,14},{14,16},{16,18},{18... | collective-permute-start | bytes 104 | tf_op jit(solution)/shard_map/ppermute | solution.py:389
  34.2 0.0 collective-permute-done.5.left1
  34.2 0.0 copy-start.3
  34.2 0.0 collective-permute-done.6.right1
  34.2 0.0 copy-start.4
  34.2 0.0 collective-permute-done.4.own1
  34.2 0.0 copy-done.1
  34.2 0.0 copy-done.2
  34.2 0.7 copy-done.3
  35.0 0.2 copy-done.4
  35.2 0.0 copy-start
  35.2 1.0 %copy-done = f32[2,1024,128]{2,1,0:T(8,128)} copy-done((f32[2,1024,128]{2,1,0:T(8,128)}, f32[2,1024,128]{2,1,0:T(8,128)S(1)}, u32[]{:S(2)}) %copy-start) | copy-done | bytes 1048600
  36.1 24.4 %waves.1 = (f32[2,2,256,128]{3,2,1,0:T(8,128)}, bf16[2,2,256,128]{3,2,1,0:T(8,128)(2,1)}, bf16[2,2,256,128]{3,2,1,0:T(8,128)(2,1)}, bf16[2,2,256,128]{3,2,1,0:T(8,128)(2,1)}) custom-call(s32[4]{0:T(128)} %rows.3, s32[4]{0:T(128)} %cols.1, s32[1]{0:T(128)S(6)} %copy.12.counts, s32[4]{0:T(128)} %dataset.1, f32[16]{0:T(128)} %dose.1, f32[16]{0:T(128)} %ground.1, ...), custom_call_target="tpu_custom_call" | custom-call | tf_op jit(solution)/shard_map/waves/pallas_call | solution.py:308
  60.6 8.1 %collective-permute-start.10 = (bf16[2,2,256,128]{3,2,1,0:T(8,128)(2,1)}, bf16[2,2,256,128]{3,2,1,0:T(8,128)(2,1)S(1)}, u32[]{:S(2)}, u32[]{:S(2)}) collective-permute-start(bf16[2,2,256,128]{3,2,1,0:T(8,128)(2,1)} %get-tuple-element.11), channel_id=1, source_target_pairs={{2,0},{4,2},{6,4},{8,6},{10,8},{12,10},{14,12},{16,14},{18,16},{20... | collective-permute-start | bytes 786440 | tf_op jit(solution)/shard_map/ppermute | solution.py:399
  68.7 1.9 %collective-permute-start.8 = (bf16[2,2,256,128]{3,2,1,0:T(8,128)(2,1)}, bf16[2,2,256,128]{3,2,1,0:T(8,128)(2,1)S(1)}, u32[]{:S(2)}, u32[]{:S(2)}) collective-permute-start(bf16[2,2,256,128]{3,2,1,0:T(8,128)(2,1)} %get-tuple-element.11), channel_id=1, source_target_pairs={{0,2},{2,4},{4,6},{6,8},{8,10},{10,12},{12,14},{14,16},{16,18},{18... | collective-permute-start | bytes 786440 | tf_op jit(solution)/shard_map/ppermute | solution.py:398
  70.6 7.1 %collective-permute-start.11 = (bf16[2,2,256,128]{3,2,1,0:T(8,128)(2,1)}, bf16[2,2,256,128]{3,2,1,0:T(8,128)(2,1)S(1)}, u32[]{:S(2)}, u32[]{:S(2)}) collective-permute-start(bf16[2,2,256,128]{3,2,1,0:T(8,128)(2,1)} %get-tuple-element.12), channel_id=1, source_target_pairs={{2,1},{3,0},{4,3},{5,2},{6,5},{7,4},{8,7},{9,6},{10,9},{11,8},{12,... | collective-permute-start | bytes 786440 | tf_op jit(solution)/shard_map/ppermute | solution.py:401
  77.7 0.0 collective-permute-done.1
  77.7 1.9 %collective-permute-start.9 = (bf16[2,2,256,128]{3,2,1,0:T(8,128)(2,1)}, bf16[2,2,256,128]{3,2,1,0:T(8,128)(2,1)S(1)}, u32[]{:S(2)}, u32[]{:S(2)}) collective-permute-start(bf16[2,2,256,128]{3,2,1,0:T(8,128)(2,1)} %get-tuple-element.12), channel_id=1, source_target_pairs={{0,3},{1,2},{2,5},{3,4},{4,7},{5,6},{6,9},{7,8},{8,11},{9,10},{10,... | collective-permute-start | bytes 786440 | tf_op jit(solution)/shard_map/ppermute | solution.py:400
  79.7 0.0 collective-permute-done
  79.7 1.3 %collective-permute-start.7 = (bf16[2,2,256,128]{3,2,1,0:T(8,128)(2,1)}, bf16[2,2,256,128]{3,2,1,0:T(8,128)(2,1)S(1)}, u32[]{:S(2)}, u32[]{:S(2)}) collective-permute-start(bf16[2,2,256,128]{3,2,1,0:T(8,128)(2,1)} %get-tuple-element.10), channel_id=1, source_target_pairs={{0,1},{1,0},{2,3},{3,2},{4,5},{5,4},{6,7},{7,6},{8,9},{9,8},{10,11... | collective-permute-start | bytes 786440 | tf_op jit(solution)/shard_map/ppermute | solution.py:397
  80.9 0.6 slice_bitcast_fusion
  81.5 0.6 slice_bitcast_fusion.2
  82.1 0.0 collective-permute-done.10.rr0
  82.1 0.0 copy-start.5
  82.1 2.1 %collective-permute-done.11.rr1 = bf16[2,2,256,128]{3,2,1,0:T(8,128)(2,1)S(1)} collective-permute-done((bf16[2,2,256,128]{3,2,1,0:T(8,128)(2,1)}, bf16[2,2,256,128]{3,2,1,0:T(8,128)(2,1)S(1)}, u32[]{:S(2)}, u32[]{:S(2)}) %collective-permute-start.11) | collective-permute-done | bytes 262176 | tf_op jit(solution)/shard_map/ppermute | solution.py:401
  84.2 0.0 copy-start.7
  84.2 0.0 collective-permute-done.8.ll0
  84.2 0.0 copy-start.6
  84.2 7.1 %collective-permute-done.9.ll1 = bf16[2,2,256,128]{3,2,1,0:T(8,128)(2,1)S(1)} collective-permute-done((bf16[2,2,256,128]{3,2,1,0:T(8,128)(2,1)}, bf16[2,2,256,128]{3,2,1,0:T(8,128)(2,1)S(1)}, u32[]{:S(2)}, u32[]{:S(2)}) %collective-permute-start.9) | collective-permute-done | bytes 262176 | tf_op jit(solution)/shard_map/ppermute | solution.py:400
  91.3 0.0 copy-start.8
  91.3 0.0 collective-permute-done.7.theirs
  91.3 0.0 copy-start.9
  91.3 0.0 copy-done.5
  91.3 0.0 copy-done.7
  91.3 0.0 copy-done.6
  91.4 0.7 copy-done.8
  92.0 0.1 copy-done.9
  92.1 2.8 %combine.1 = f32[2,1024,128]{2,1,0:T(8,128)} custom-call(s32[4]{0:T(128)} %rows.3, s32[4]{0:T(128)} %get-tuple-element.16.lrows, s32[4]{0:T(128)} %get-tuple-element.15.lcols, s32[4]{0:T(128)} %get-tuple-element.14.rrows, s32[4]{0:T(128)} %get-tuple-element.13.rcols, f32[2,2,256,128]{3,2,1,0:T(8,128)} %get-tuple-element.9.mine, ...), custom_call_target="tpu_custom_call" | custom-call | tf_op jit(solution)/shard_map/combine/pallas_call | solution.py:364
Async XLA Ops:
  1.3 19.8 %collective-permute-start.2 = (bf16[2,1024,128]{2,1,0:T(8,128)(2,1)S(1)}, bf16[2,1024,128]{2,1,0:T(8,128)(2,1)S(1)}, u32[]{:S(2)}, u32[]{:S(2)}) collective-permute-start(bf16[2,1024,128]{2,1,0:T(8,128)(2,1)S(1)} %bitcast_convert_fusion), channel_id=1, source_target_pairs={{0,2},{2,4},{4,6},{6,8},{8,10},{10,12},{12,14},{14,16},{16,18},{18... | collective-permute-start | bytes 1572872 | tf_op jit(solution)/shard_map/ppermute | solution.py:383
  4.7 17.6 %collective-permute-start.3 = (bf16[2,1024,128]{2,1,0:T(8,128)(2,1)S(1)}, bf16[2,1024,128]{2,1,0:T(8,128)(2,1)S(1)}, u32[]{:S(2)}, u32[]{:S(2)}) collective-permute-start(bf16[2,1024,128]{2,1,0:T(8,128)(2,1)S(1)} %bitcast_convert_fusion), channel_id=1, source_target_pairs={{2,0},{4,2},{6,4},{8,6},{10,8},{12,10},{14,12},{16,14},{18,16},{20... | collective-permute-start | bytes 1572872 | tf_op jit(solution)/shard_map/ppermute | solution.py:384
  11.4 22.8 %collective-permute-start.4 = (f32[2,1024,128]{2,1,0:T(8,128)}, f32[2,1024,128]{2,1,0:T(8,128)S(1)}, u32[]{:S(2)}, u32[]{:S(2)}) collective-permute-start(f32[2,1024,128]{2,1,0:T(8,128)} %bitcast.13), channel_id=1, source_target_pairs={{0,1},{1,0},{2,3},{3,2},{4,5},{5,4},{6,7},{7,6},{8,9},{9,8},{10,11... | collective-permute-start | bytes 3145736 | tf_op jit(solution)/shard_map/ppermute | solution.py:385
  21.1 13.1 %copy-start.1 = (bf16[2,1024,128]{2,1,0:T(8,128)(2,1)}, bf16[2,1024,128]{2,1,0:T(8,128)(2,1)S(1)}, u32[]{:S(2)}) copy-start(bf16[2,1024,128]{2,1,0:T(8,128)(2,1)S(1)} %collective-permute-done.2.left0) | copy-start | bytes 1572868
  21.1 13.1 %collective-permute-start.5 = (bf16[2,1024,128]{2,1,0:T(8,128)(2,1)S(1)}, bf16[2,1024,128]{2,1,0:T(8,128)(2,1)S(1)}, u32[]{:S(2)}, u32[]{:S(2)}) collective-permute-start(bf16[2,1024,128]{2,1,0:T(8,128)(2,1)S(1)} %collective-permute-done.2.left0), channel_id=1, source_target_pairs={{0,1},{1,0},{2,3},{3,2},{4,5},{5,4},{6,7},{7,6},{8,9},{9,8},{10,11... | collective-permute-start | bytes 1572872 | tf_op jit(solution)/shard_map/ppermute | solution.py:386
  22.3 12.0 %copy-start.2 = (bf16[2,1024,128]{2,1,0:T(8,128)(2,1)}, bf16[2,1024,128]{2,1,0:T(8,128)(2,1)S(1)}, u32[]{:S(2)}) copy-start(bf16[2,1024,128]{2,1,0:T(8,128)(2,1)S(1)} %collective-permute-done.3.right0) | copy-start | bytes 1572868
  22.3 11.9 %collective-permute-start.6 = (bf16[2,1024,128]{2,1,0:T(8,128)(2,1)S(1)}, bf16[2,1024,128]{2,1,0:T(8,128)(2,1)S(1)}, u32[]{:S(2)}, u32[]{:S(2)}) collective-permute-start(bf16[2,1024,128]{2,1,0:T(8,128)(2,1)S(1)} %collective-permute-done.3.right0), channel_id=1, source_target_pairs={{0,1},{1,0},{2,3},{3,2},{4,5},{5,4},{6,7},{7,6},{8,9},{9,8},{10,11... | collective-permute-start | bytes 1572872 | tf_op jit(solution)/shard_map/ppermute | solution.py:387
  23.0 54.7 %collective-permute-start.1 = (s32[2,4]{1,0:T(2,128)S(1)}, s32[2,4]{1,0:T(2,128)S(1)}, u32[]{:S(2)}, u32[]{:S(2)}) collective-permute-start(s32[2,4]{1,0:T(2,128)S(1)} %pad_add_fusion), channel_id=1, source_target_pairs={{2,0},{4,2},{6,4},{8,6},{10,8},{12,10},{14,12},{16,14},{18,16},{20... | collective-permute-start | bytes 104 | tf_op jit(solution)/shard_map/ppermute | solution.py:390
  31.6 48.1 %collective-permute-start = (s32[2,4]{1,0:T(2,128)S(1)}, s32[2,4]{1,0:T(2,128)S(1)}, u32[]{:S(2)}, u32[]{:S(2)}) collective-permute-start(s32[2,4]{1,0:T(2,128)S(1)} %pad_add_fusion), channel_id=1, source_target_pairs={{0,2},{2,4},{4,6},{6,8},{8,10},{10,12},{12,14},{14,16},{16,18},{18... | collective-permute-start | bytes 104 | tf_op jit(solution)/shard_map/ppermute | solution.py:389
  34.2 0.8 copy-start.3
  34.2 1.0 %copy-start.4 = (bf16[2,1024,128]{2,1,0:T(8,128)(2,1)}, bf16[2,1024,128]{2,1,0:T(8,128)(2,1)S(1)}, u32[]{:S(2)}) copy-start(bf16[2,1024,128]{2,1,0:T(8,128)(2,1)S(1)} %collective-permute-done.6.right1) | copy-start | bytes 1572868
  35.2 1.0 %copy-start = (f32[2,1024,128]{2,1,0:T(8,128)}, f32[2,1024,128]{2,1,0:T(8,128)S(1)}, u32[]{:S(2)}) copy-start(f32[2,1024,128]{2,1,0:T(8,128)S(1)} %collective-permute-done.4.own1) | copy-start | bytes 3145732
  60.6 21.5 %collective-permute-start.10 = (bf16[2,2,256,128]{3,2,1,0:T(8,128)(2,1)}, bf16[2,2,256,128]{3,2,1,0:T(8,128)(2,1)S(1)}, u32[]{:S(2)}, u32[]{:S(2)}) collective-permute-start(bf16[2,2,256,128]{3,2,1,0:T(8,128)(2,1)} %get-tuple-element.11), channel_id=1, source_target_pairs={{2,0},{4,2},{6,4},{8,6},{10,8},{12,10},{14,12},{16,14},{18,16},{20... | collective-permute-start | bytes 786440 | tf_op jit(solution)/shard_map/ppermute | solution.py:399
  68.7 15.5 %collective-permute-start.8 = (bf16[2,2,256,128]{3,2,1,0:T(8,128)(2,1)}, bf16[2,2,256,128]{3,2,1,0:T(8,128)(2,1)S(1)}, u32[]{:S(2)}, u32[]{:S(2)}) collective-permute-start(bf16[2,2,256,128]{3,2,1,0:T(8,128)(2,1)} %get-tuple-element.11), channel_id=1, source_target_pairs={{0,2},{2,4},{4,6},{6,8},{8,10},{10,12},{12,14},{14,16},{16,18},{18... | collective-permute-start | bytes 786440 | tf_op jit(solution)/shard_map/ppermute | solution.py:398
  70.6 13.6 %collective-permute-start.11 = (bf16[2,2,256,128]{3,2,1,0:T(8,128)(2,1)}, bf16[2,2,256,128]{3,2,1,0:T(8,128)(2,1)S(1)}, u32[]{:S(2)}, u32[]{:S(2)}) collective-permute-start(bf16[2,2,256,128]{3,2,1,0:T(8,128)(2,1)} %get-tuple-element.12), channel_id=1, source_target_pairs={{2,1},{3,0},{4,3},{5,2},{6,5},{7,4},{8,7},{9,6},{10,9},{11,8},{12,... | collective-permute-start | bytes 786440 | tf_op jit(solution)/shard_map/ppermute | solution.py:401
  77.7 13.6 %collective-permute-start.9 = (bf16[2,2,256,128]{3,2,1,0:T(8,128)(2,1)}, bf16[2,2,256,128]{3,2,1,0:T(8,128)(2,1)S(1)}, u32[]{:S(2)}, u32[]{:S(2)}) collective-permute-start(bf16[2,2,256,128]{3,2,1,0:T(8,128)(2,1)} %get-tuple-element.12), channel_id=1, source_target_pairs={{0,3},{1,2},{2,5},{3,4},{4,7},{5,6},{6,9},{7,8},{8,11},{9,10},{10,... | collective-permute-start | bytes 786440 | tf_op jit(solution)/shard_map/ppermute | solution.py:400
  79.7 11.6 %collective-permute-start.7 = (bf16[2,2,256,128]{3,2,1,0:T(8,128)(2,1)}, bf16[2,2,256,128]{3,2,1,0:T(8,128)(2,1)S(1)}, u32[]{:S(2)}, u32[]{:S(2)}) collective-permute-start(bf16[2,2,256,128]{3,2,1,0:T(8,128)(2,1)} %get-tuple-element.10), channel_id=1, source_target_pairs={{0,1},{1,0},{2,3},{3,2},{4,5},{5,4},{6,7},{7,6},{8,9},{9,8},{10,11... | collective-permute-start | bytes 786440 | tf_op jit(solution)/shard_map/ppermute | solution.py:397
  82.1 9.2 %copy-start.5 = (bf16[2,2,256,128]{3,2,1,0:T(8,128)(2,1)}, bf16[2,2,256,128]{3,2,1,0:T(8,128)(2,1)S(1)}, u32[]{:S(2)}) copy-start(bf16[2,2,256,128]{3,2,1,0:T(8,128)(2,1)S(1)} %collective-permute-done.10.rr0) | copy-start | bytes 786436
  84.2 7.1 %copy-start.7 = (bf16[2,2,256,128]{3,2,1,0:T(8,128)(2,1)}, bf16[2,2,256,128]{3,2,1,0:T(8,128)(2,1)S(1)}, u32[]{:S(2)}) copy-start(bf16[2,2,256,128]{3,2,1,0:T(8,128)(2,1)S(1)} %collective-permute-done.11.rr1) | copy-start | bytes 786436
  84.2 7.1 %copy-start.6 = (bf16[2,2,256,128]{3,2,1,0:T(8,128)(2,1)}, bf16[2,2,256,128]{3,2,1,0:T(8,128)(2,1)S(1)}, u32[]{:S(2)}) copy-start(bf16[2,2,256,128]{3,2,1,0:T(8,128)(2,1)S(1)} %collective-permute-done.8.ll0) | copy-start | bytes 786436
  91.3 0.7 copy-start.8
  91.3 0.8 copy-start.9

commit v2 on v1

v2 whole, which is shorter than its diff:
```python
import functools
import math

import jax
import jax.numpy as jnp
import numpy as np
from jax import lax
from jax.experimental import pallas as pl
from jax.experimental.pallas import tpu as pltpu
from jax.sharding import PartitionSpec as P

L = 256
Q = 128
MODES = 6
GROUP = 3
SLOTS = 2
ROWS = 1024
BF = jnp.bfloat16
F32 = jnp.float32
VMEM = pltpu.VMEM
SMEM = pltpu.SMEM


def rounded(values):
    return np.asarray(values, np.float32).astype(jnp.bfloat16).astype(np.float64)


def block(values):
    re, im = values.real, values.imag
    full = np.block([[re, -im], [im, re]])
    return np.stack([full, full.T])


@functools.cache
def tables():
    k = np.arange(L)
    dft = np.exp(-2j * np.pi / L * (k[:, None] * k[None, :] % L)) / math.sqrt(L)
    signed = np.where(k < Q, k, k - L)
    filt = np.exp(-1j * np.pi / L * (signed * signed % (2 * L)))
    prop = dft.conj() @ (filt[:, None] * dft)
    prop = rounded(prop.real) + 1j * rounded(prop.imag)
    dft = rounded(dft.real) + 1j * rounded(dft.imag)
    near, far = prop[:Q, :Q], prop[:Q, Q:]
    halves = [(near + far) / 2, (near - far) / 2]
    kinds = [[block(h) for h in halves], [block(dft[0::2, :Q]), block(dft[1::2, :Q])]]
    return np.stack([np.stack(kind) for kind in kinds]).astype(np.float32)


@functools.cache
def lane_split():
    k = np.arange(L)
    return (k[:, None] == np.where(k < Q, 2 * k, 2 * (k - Q) + 1)[None, :]).astype(np.float32)


def dot(a, b):
    return jnp.dot(a, b, preferred_element_type=F32)


def hadamard(q):
    s0, d0 = q[0][0] + q[0][1], q[0][0] - q[0][1]
    s1, d1 = q[1][0] + q[1][1], q[1][0] - q[1][1]
    return [[s0 + s1, d0 + d1], [s0 - s1, d0 - d1]]


def quads(fn):
    return [[fn(i, j) for j in range(2)] for i in range(2)]


CH = 16


def store_waves(z_ref, m, r, re, im):
    for i in range(2):
        for j in range(2):
            z_ref[m, i, r : r + CH, Q * j : Q * j + Q] = re[i][j].astype(BF)
            z_ref[m, i, Q + r : Q + r + CH, Q * j : Q * j + Q] = im[i][j].astype(BF)


def left_side(table, kind, back, z_ref, u_ref, m):
    for i in range(2):
        u = dot(table[kind, i, back], z_ref[m, i]).astype(BF)
        for j in range(2):
            u_ref[m, j, Q * i : Q * i + Q, 0:Q] = u[0:Q, Q * j : Q * j + Q]
            u_ref[m, j, Q * i : Q * i + Q, Q:L] = u[Q:L, Q * j : Q * j + Q]


def right_side(table, kind, back, u_ref, w_ref, m):
    for j in range(2):
        w_ref[m, j] = dot(u_ref[m, j], table[kind, j, 1 - back])


def read_waves(w_ref, m, r):
    re = quads(lambda i, j: w_ref[m, j, Q * i + r : Q * i + r + CH, 0:Q])
    im = quads(lambda i, j: w_ref[m, j, Q * i + r : Q * i + r + CH, Q:L])
    return re, im


def rotate_probe(probe, pr_ref, spin, p, col):
    shift = lax.broadcasted_iota(jnp.int32, (L, L), 1) - lax.broadcasted_iota(jnp.int32, (L, L), 0)
    spin[...] = jnp.where((shift == col) | (shift == col - L), 1.0, 0.0).astype(BF)

    def one(m, _):
        for c in range(2):
            x = probe[m, c]
            hi = x.astype(BF)
            lo = (x - hi.astype(F32)).astype(BF)
            pr_ref[p, m, c] = dot(hi, spin[...]) + dot(lo, spin[...])
        return 0

    lax.fori_loop(0, MODES, one, 0)


def widen(halo, wide):
    for side in range(2):
        for c in range(2):
            wide[side, c] = halo[side, c].astype(F32)


def load_patch(own, wide, o_ref, place, row, col, first, last):
    lane = lax.broadcasted_iota(jnp.int32, (L, Q), 1)
    right = lane < col
    empty = jnp.where(right, last, first) > 0
    for c in range(2):
        halo = jnp.where(right, wide[1, c, pl.ds(row, L), :], wide[0, c, pl.ds(row, L), :])
        o_ref[place, c, :, 0:Q] = jnp.where(empty, 0.0, halo)
        o_ref[place, c, :, Q:L] = own[c, pl.ds(row, L), :]


def amplitudes(measured, slot, split, amp_ref, tmp_ref):
    for j in range(2):
        tmp_ref[j] = jnp.sqrt(measured[slot, :, Q * j : Q * j + Q])
    for i in range(2):
        x = jnp.concatenate([tmp_ref[j, pl.ds(i, Q, stride=2), :] for j in range(2)], axis=1)
        hi = x.astype(BF)
        rest = x - hi.astype(F32)
        mid = rest.astype(BF)
        lo = (rest - mid.astype(F32)).astype(BF)
        amp_ref[i] = dot(hi, split[...]) + (dot(mid, split[...]) + dot(lo, split[...]))


def forward_first(table, pr_ref, o_ref, p, z, u, w, psi_ref):
    def group(g, _):
        for k in range(GROUP):
            m = g * GROUP + k
            for r in range(0, Q, CH):
                re, im = [[None] * 2 for _ in range(2)], [[None] * 2 for _ in range(2)]
                for i in range(2):
                    for j in range(2):
                        rows, lanes = slice(Q * i + r, Q * i + r + CH), slice(Q * j, Q * j + Q)
                        a, b = pr_ref[p, m, 0, rows, lanes], pr_ref[p, m, 1, rows, lanes]
                        c, d = o_ref[2 * p, 0, rows, lanes], o_ref[2 * p, 1, rows, lanes]
                        re[i][j], im[i][j] = a * c - b * d, a * d + b * c
                store_waves(z, k, r, hadamard(re), hadamard(im))
        for k in range(GROUP):
            left_side(table, 0, 0, z, u, k)
        for k in range(GROUP):
            right_side(table, 0, 0, u, w, k)
        for k in range(GROUP):
            m = g * GROUP + k
            for r in range(0, Q, CH):
                vre, vim = read_waves(w, k, r)
                vre, vim = hadamard(vre), hadamard(vim)
                for i in range(2):
                    for j in range(2):
                        rows, lanes = slice(Q * i + r, Q * i + r + CH), slice(Q * j, Q * j + Q)
                        psi_ref[p, m, 0, rows, lanes] = vre[i][j].astype(BF)
                        psi_ref[p, m, 1, rows, lanes] = vim[i][j].astype(BF)
        return 0

    lax.fori_loop(0, MODES // GROUP, group, 0)


def forward_last(table, o_ref, p, z, u, psi_ref, far_ref, int_ref):
    int_ref[...] = jnp.zeros_like(int_ref)

    def group(g, _):
        for k in range(GROUP):
            m = g * GROUP + k
            for r in range(0, Q, CH):
                re, im = [[None] * 2 for _ in range(2)], [[None] * 2 for _ in range(2)]
                for i in range(2):
                    for j in range(2):
                        rows, lanes = slice(Q * i + r, Q * i + r + CH), slice(Q * j, Q * j + Q)
                        a = psi_ref[p, m, 0, rows, lanes].astype(F32)
                        b = psi_ref[p, m, 1, rows, lanes].astype(F32)
                        c, d = o_ref[2 * p + 1, 0, rows, lanes], o_ref[2 * p + 1, 1, rows, lanes]
                        re[i][j], im[i][j] = a * c - b * d, a * d + b * c
                store_waves(z, k, r, hadamard(re), hadamard(im))
        for k in range(GROUP):
            left_side(table, 1, 0, z, u, k)
        for k in range(GROUP):
            for j in range(2):
                far_ref[g * GROUP + k, j] = dot(u[k, j], table[1, j, 1])
        for j in range(2):
            for r in range(0, L, CH):
                total = int_ref[j, r : r + CH, :]
                for k in range(GROUP):
                    x = far_ref[g * GROUP + k, j, r : r + CH, 0:Q]
                    y = far_ref[g * GROUP + k, j, r : r + CH, Q:L]
                    total = total + (x * x + y * y)
                int_ref[j, r : r + CH, :] = total
        return 0

    lax.fori_loop(0, MODES // GROUP, group, 0)


def residual_factor(int_ref, amp_ref, fac_ref, scale, offset, valid):
    for j in range(2):
        for i in range(2):
            intensity = scale * int_ref[j, Q * i : Q * i + Q, :] + offset
            ratio = amp_ref[i, :, Q * j : Q * j + Q] / jnp.sqrt(intensity)
            fac_ref[j, Q * i : Q * i + Q, :] = jnp.where(valid, scale * (1.0 - ratio), 0.0)


def conj_terms(grad_ref, place, r, terms):
    for i in range(2):
        for j in range(2):
            rows, lanes = slice(Q * i + r, Q * i + r + CH), slice(Q * j, Q * j + Q)
            gre, gim = grad_ref[place, 0, rows, lanes], grad_ref[place, 1, rows, lanes]
            a, b, x, y = terms(i, j, rows, lanes)
            grad_ref[place, 0, rows, lanes] = gre + (a * x + b * y)
            grad_ref[place, 1, rows, lanes] = gim + (a * y - b * x)


def backward_last(table, o_ref, p, z, u, w, psi_ref, far_ref, fac_ref, grad_ref, gz_ref):
    grad_ref[2 * p + 1] = jnp.zeros((2, L, L), F32)

    def group(g, _):
        for k in range(GROUP):
            m = g * GROUP + k
            for j in range(2):
                for r in range(0, L, CH):
                    f = fac_ref[j, r : r + CH, :]
                    i, s = r // Q, r % Q
                    z[k, i, s : s + CH, Q * j : Q * j + Q] = (f * far_ref[m, j, r : r + CH, 0:Q]).astype(BF)
                    z[k, i, Q + s : Q + s + CH, Q * j : Q * j + Q] = (
                        f * far_ref[m, j, r : r + CH, Q:L]
                    ).astype(BF)
        for k in range(GROUP):
            left_side(table, 1, 1, z, u, k)
        for k in range(GROUP):
            right_side(table, 1, 1, u, w, k)
        for k in range(GROUP):
            m = g * GROUP + k
            for r in range(0, Q, CH):
                vre, vim = read_waves(w, k, r)
                vre, vim = hadamard(vre), hadamard(vim)
                conj_terms(
                    grad_ref,
                    2 * p + 1,
                    r,
                    lambda i, j, rows, lanes: (
                        psi_ref[p, m, 0, rows, lanes].astype(F32),
                        psi_ref[p, m, 1, rows, lanes].astype(F32),
                        vre[i][j],
                        vim[i][j],
                    ),
                )
                re, im = [[None] * 2 for _ in range(2)], [[None] * 2 for _ in range(2)]
                for i in range(2):
                    for j in range(2):
                        rows, lanes = slice(Q * i + r, Q * i + r + CH), slice(Q * j, Q * j + Q)
                        c, d = o_ref[2 * p + 1, 0, rows, lanes], o_ref[2 * p + 1, 1, rows, lanes]
                        x, y = vre[i][j], vim[i][j]
                        re[i][j], im[i][j] = c * x + d * y, c * y - d * x
                store_waves(gz_ref, m, r, hadamard(re), hadamard(im))
        return 0

    lax.fori_loop(0, MODES // GROUP, group, 0)


def backward_first(table, pr_ref, p, u, w, grad_ref, gz_ref):
    grad_ref[2 * p] = jnp.zeros((2, L, L), F32)

    def group(g, _):
        for k in range(GROUP):
            m = g * GROUP + k
            for i in range(2):
                x = dot(table[0, i, 1], gz_ref[m, i]).astype(BF)
                for j in range(2):
                    u[k, j, Q * i : Q * i + Q, 0:Q] = x[0:Q, Q * j : Q * j + Q]
                    u[k, j, Q * i : Q * i + Q, Q:L] = x[Q:L, Q * j : Q * j + Q]
        for k in range(GROUP):
            right_side(table, 0, 1, u, w, k)
        for k in range(GROUP):
            m = g * GROUP + k
            for r in range(0, Q, CH):
                vre, vim = read_waves(w, k, r)
                vre, vim = hadamard(vre), hadamard(vim)
                conj_terms(
                    grad_ref,
                    2 * p,
                    r,
                    lambda i, j, rows, lanes: (
                        pr_ref[p, m, 0, rows, lanes],
                        pr_ref[p, m, 1, rows, lanes],
                        vre[i][j],
                        vim[i][j],
                    ),
                )
        return 0

    lax.fori_loop(0, MODES // GROUP, group, 0)


CHUNKS = 4
MESH = pl.DeviceIdType.MESH


def wave_kernel(
    rows, cols, counts, dataset, dose, ground,
    trans, probe_in, measured_in, table_in, split_in,
    own_mine, own_in, halo_in, places_in,
    own_a, own_b, halo_a, halo_b, short, places, own_out, halo_out,
    probe, measured, table, split, spin,
    o_ref, pr_ref, psi_ref, far_ref, int_ref, fac_ref, amp_ref, z, u, w, gz, grad_ref, wide,
    load_sem, own_send, own_recv, side_send, side_recv, relay_send, relay_recv,
    place_send, place_recv, grad_send, grad_recv, part_send, part_recv, go,
):
    depth = lax.axis_index("depth")
    tile = lax.axis_index("tile")
    tiles = lax.axis_size("tile")
    ahead, behind = lax.rem(tile + 1, tiles), lax.rem(tile + tiles - 1, tiles)
    other = 1 - depth
    beside = (ahead, behind)

    barrier = pltpu.get_barrier_semaphore()
    for target in ((ahead, depth), (behind, depth), (ahead, other), (behind, other), (tile, other)):
        pl.semaphore_signal(barrier, inc=1, device_id=target, device_id_type=MESH)

    def remote(src, dst, send, recv, target):
        return pltpu.make_async_remote_copy(
            src_ref=src, dst_ref=dst, send_sem=send, recv_sem=recv, device_id=target, device_id_type=MESH
        )

    loads = [
        pltpu.make_async_copy(probe_in, probe, load_sem.at[0]),
        pltpu.make_async_copy(measured_in.at[pl.ds(depth * SLOTS, SLOTS)], measured, load_sem.at[1]),
        pltpu.make_async_copy(table_in, table, load_sem.at[2]),
        pltpu.make_async_copy(split_in, split, load_sem.at[3]),
    ]

    def own_load(ref):
        return pltpu.make_async_copy(trans.at[0], ref, load_sem.at[4])

    def own_copy(ref):
        return remote(trans.at[0], ref, own_send, own_recv, (tile, other))

    def side_copy(ref, side, k):
        span = pl.ds(k * (ROWS // CHUNKS), ROWS // CHUNKS)
        return remote(
            short.at[:, span, :], ref.at[side, :, span, :], side_send.at[side, k], side_recv.at[side, k],
            (beside[side], depth),
        )

    def relay_copy(ref, side, k):
        span = pl.ds(k * (ROWS // CHUNKS), ROWS // CHUNKS)
        return remote(
            ref.at[side, :, span, :], ref.at[side, :, span, :], relay_send.at[side, k], relay_recv.at[side, k],
            (tile, other),
        )

    def place_copy(side):
        return remote(places, places_in.at[side], place_send.at[side], place_recv.at[side], (beside[side], depth))

    def grad_copy(p, home, side):
        target = depth if home == 0 else other
        return remote(
            halo_out.at[p, home], halo_in.at[side, depth, p], grad_send.at[p, home, side],
            grad_recv.at[side, depth, p], (beside[side], target),
        )

    def grad_arrival(p, core, side):
        return remote(
            halo_out.at[p, 0], halo_in.at[side, core, p], grad_send.at[p, 0, side], grad_recv.at[side, core, p],
            (beside[side], depth),
        )

    def part_copy(p):
        return remote(own_out.at[p], own_in.at[p], part_send.at[p], part_recv.at[p], (tile, other))

    mine = {0: (own_a, halo_a), 1: (own_b, halo_b)}
    for d in range(2):
        @pl.when(depth == d)
        def _():
            own_load(mine[d][0]).start()
    for load in loads:
        load.start()
    for n in range(4):
        places[n : n + 1, :] = jnp.full((1, Q), rows[n], jnp.int32)
        places[n + 4 : n + 5, :] = jnp.full((1, Q), cols[n], jnp.int32)
    for d in range(2):
        @pl.when(depth == d)
        def _():
            own_load(mine[d][0]).wait()
            for c in range(2):
                short[c] = mine[d][0][c].astype(BF)
    pl.semaphore_wait(barrier, 5)

    for d in range(2):
        @pl.when(depth == d)
        def _():
            own_copy(mine[d][0]).start()
    @pl.when(depth == 0)
    def _():
        for k in range(CHUNKS):
            for side in range(2):
                side_copy(halo_a, side, k).start()
    for side in range(2):
        place_copy(side).start()

    def spot(p):
        slot = depth * SLOTS + p
        return slot, jnp.clip(rows[slot], 0, ROWS - L), jnp.clip(cols[slot], 0, Q - 1)

    loads[0].wait()

    def turn(p, _):
        rotate_probe(probe, pr_ref, spin, p, spot(p)[2])
        return 0

    lax.fori_loop(0, SLOTS, turn, 0)
    for load in loads[1:]:
        load.wait()

    @pl.when(depth == 0)
    def _():
        for k in range(CHUNKS):
            for side in range(2):
                side_copy(halo_a, side, k).wait_recv()
                relay_copy(halo_a, side, k).start()
        for k in range(CHUNKS):
            for side in range(2):
                side_copy(halo_a, side, k).wait_send()
        pl.semaphore_signal(go, inc=1, device_id=(tile, other), device_id_type=MESH)
        own_copy(own_b).wait_recv()

    @pl.when(depth == 1)
    def _():
        pl.semaphore_wait(go, 1)
        for k in range(CHUNKS):
            for side in range(2):
                side_copy(halo_b, side, k).start()
        own_copy(own_a).wait_recv()
        for k in range(CHUNKS):
            for side in range(2):
                relay_copy(halo_a, side, k).wait_recv()
    own_copy(own_a).wait_send()
    widen(halo_a, wide)

    first = (tile == 0).astype(jnp.int32)
    last = (tile == tiles - 1).astype(jnp.int32)

    def start(p, _):
        _, row, col = spot(p)
        load_patch(own_a, wide, o_ref, 2 * p, row, col, first, last)
        forward_first(table, pr_ref, o_ref, p, z, u, w, psi_ref)

        @pl.when(depth == 1)
        def _():
            for kk in range(CHUNKS // SLOTS):
                for side in range(2):
                    k = p * (CHUNKS // SLOTS) + kk
                    side_copy(halo_b, side, k).wait_recv()
                    relay_copy(halo_b, side, k).start()
        return 0

    lax.fori_loop(0, SLOTS, start, 0)

    @pl.when(depth == 0)
    def _():
        for k in range(CHUNKS):
            for side in range(2):
                relay_copy(halo_b, side, k).wait_recv()
                relay_copy(halo_a, side, k).wait_send()

    @pl.when(depth == 1)
    def _():
        for k in range(CHUNKS):
            for side in range(2):
                side_copy(halo_b, side, k).wait_send()
                relay_copy(halo_b, side, k).wait_send()

    widen(halo_b, wide)

    def hand_over(p, s):
        place = 2 * p + s
        @pl.when(depth == s)
        def _():
            own_mine[p] = grad_ref[place, :, :, Q:L]
            halo_out[p, 0] = grad_ref[place, :, :, 0:Q].astype(BF)
            for side in range(2):
                grad_copy(p, 0, side).start()
        @pl.when(depth != s)
        def _():
            own_out[p] = grad_ref[place, :, :, Q:L].astype(BF)
            halo_out[p, 1] = grad_ref[place, :, :, 0:Q].astype(BF)
            for side in range(2):
                grad_copy(p, 1, side).start()
            part_copy(p).start()

    def finish(p, _):
        slot, row, col = spot(p)
        which = jnp.clip(dataset[slot], 0, dose.shape[0] - 1)
        load_patch(own_b, wide, o_ref, 2 * p + 1, row, col, first, last)
        amplitudes(measured, p, split, amp_ref, int_ref)
        forward_last(table, o_ref, p, z, u, psi_ref, far_ref, int_ref)
        residual_factor(int_ref, amp_ref, fac_ref, dose[which], ground[which], slot < counts[0])
        backward_last(table, o_ref, p, z, u, w, psi_ref, far_ref, fac_ref, grad_ref, gz)
        hand_over(p, 1)
        backward_first(table, pr_ref, p, u, w, grad_ref, gz)
        hand_over(p, 0)
        return 0

    lax.fori_loop(0, SLOTS, finish, 0)

    for side in range(2):
        place_copy(side).wait()
    for p in range(SLOTS):
        part_copy(p).wait()
        for side in range(2):
            for home in range(2):
                grad_copy(p, home, side).wait_send()
            for core in range(2):
                grad_arrival(p, core, side).wait_recv()


def waves(scalars, transmission, probe, measured):
    vm = pl.BlockSpec(memory_space=VMEM)
    hbm = pl.BlockSpec(memory_space=pltpu.HBM)
    dma = pltpu.SemaphoreType.DMA
    return pl.pallas_call(
        wave_kernel,
        out_shape=(
            jax.ShapeDtypeStruct((SLOTS, 2, L, Q), F32),
            jax.ShapeDtypeStruct((SLOTS, 2, L, Q), BF),
            jax.ShapeDtypeStruct((2, 2, SLOTS, 2, L, Q), BF),
            jax.ShapeDtypeStruct((2, 8, Q), jnp.int32),
        ),
        in_specs=[pl.BlockSpec(memory_space=SMEM)] * 6 + [hbm] * 5,
        out_specs=(vm,) * 4,
        scratch_shapes=[
            VMEM((2, ROWS, Q), F32),
            VMEM((2, ROWS, Q), F32),
            VMEM((2, 2, ROWS, Q), BF),
            VMEM((2, 2, ROWS, Q), BF),
            VMEM((2, ROWS, Q), BF),
            VMEM((8, Q), jnp.int32),
            VMEM((SLOTS, 2, L, Q), BF),
            VMEM((SLOTS, 2, 2, L, Q), BF),
            VMEM((MODES, 2, L, L), F32),
            VMEM((SLOTS, L, L), F32),
            VMEM((2, 2, 2, L, L), BF),
            VMEM((L, L), BF),
            VMEM((L, L), BF),
            VMEM((4, 2, L, L), F32),
            VMEM((SLOTS, MODES, 2, L, L), F32),
            VMEM((SLOTS, MODES, 2, L, L), BF),
            VMEM((MODES, 2, L, L), F32),
            VMEM((2, L, Q), F32),
            VMEM((2, L, Q), F32),
            VMEM((2, Q, L), F32),
            VMEM((GROUP, 2, L, L), BF),
            VMEM((GROUP, 2, L, L), BF),
            VMEM((GROUP, 2, L, L), F32),
            VMEM((MODES, 2, L, L), BF),
            VMEM((4, 2, L, L), F32),
            VMEM((2, 2, ROWS, Q), F32),
            dma((5,)),
            dma(()),
            dma(()),
            dma((2, CHUNKS)),
            dma((2, CHUNKS)),
            dma((2, CHUNKS)),
            dma((2, CHUNKS)),
            dma((2,)),
            dma((2,)),
            dma((SLOTS, 2, 2)),
            dma((2, 2, SLOTS)),
            dma((SLOTS,)),
            dma((SLOTS,)),
            pltpu.SemaphoreType.REGULAR,
        ],
        compiler_params=pltpu.CompilerParams(
            vmem_limit_bytes=60 * 2**20, collective_id=0, has_side_effects=True
        ),
        name="waves",
    )(
        *scalars,
        transmission,
        probe,
        measured,
        jnp.asarray(tables()).astype(BF),
        jnp.asarray(lane_split()).astype(BF),
    )


def combine_kernel(rows, places, mine, theirs, halo, out):
    depth = lax.axis_index("depth")
    tile = lax.axis_index("tile")
    lane = lax.broadcasted_iota(jnp.int32, (L, Q), 1)
    out[...] = jnp.zeros_like(out)

    def add(row, values):
        row = jnp.clip(row, 0, ROWS - L)
        for c in range(2):
            out[c, pl.ds(row, L), :] += values(c)

    for p in range(SLOTS):
        add(rows[depth * SLOTS + p], lambda c: mine[p, c])
        add(rows[(1 - depth) * SLOTS + p], lambda c: theirs[p, c].astype(F32))
        for core in range(2):
            slot = core * SLOTS + p

            @pl.when(tile > 0)
            def _():
                kept = lane < places[0, slot + 4, 0]
                add(places[0, slot, 0], lambda c: jnp.where(kept, halo[0, core, p, c].astype(F32), 0.0))

            @pl.when(tile < lax.axis_size("tile") - 1)
            def _():
                kept = lane >= places[1, slot + 4, 0]
                add(places[1, slot, 0], lambda c: jnp.where(kept, halo[1, core, p, c].astype(F32), 0.0))


def combine(rows, places, parts):
    vm = pl.BlockSpec(memory_space=VMEM)
    return pl.pallas_call(
        combine_kernel,
        out_shape=jax.ShapeDtypeStruct((2, ROWS, Q), F32),
        in_specs=[pl.BlockSpec(memory_space=SMEM)] * 2 + [vm] * 3,
        out_specs=vm,
        compiler_params=pltpu.CompilerParams(vmem_limit_bytes=60 * 2**20),
        name="combine",
    )(rows, places, *parts)


def shards(transmission, probe_modes, measured, scan_rows, scan_cols, counts, dataset, dose_scale, background):
    mine, theirs, halo, places = waves(
        (scan_rows, scan_cols, counts, dataset, dose_scale, background), transmission, probe_modes, measured
    )
    return combine(scan_rows, places, (mine, theirs, halo))[None]


def solution(mesh):
    in_specs = (
        P("depth", None, None, "tile"),
        P(),
        P("tile", None, None),
        P("tile"),
        P("tile"),
        P("tile"),
        P("tile"),
        P(),
        P(),
    )
    out_specs = P("depth", None, None, "tile")
    return jax.shard_map(shards, mesh=mesh, in_specs=in_specs, out_specs=out_specs, check_vma=False)
```

time: 96.6 us -> 57.3 us (0.59)
  the two profiles are of different devices: /device:TPU:96 before, /device:TPU:0 now
where the time goes in v2:
time: 57.3 us; the launch traced here: 57.2 us
  Pallas kernels  56.5 us (99%)
  between operations  0.66 us (1%)
    pallas_call x1, Pallas kernels, waves(): pl.pallas_call(wave_kernel, out_shape=(jax.ShapeDtypeStruct((SLOTS, 2, L,...  53.7 us
    pallas_call x1, Pallas kernels, combine(): pl.pallas_call(combine_kernel, out_shape=jax.ShapeDtypeStruct((2, ROWS, Q...  2.77 us

profile of v2, /device:TPU:0, one launch (start us, length us, event | category | flops | bytes accessed | tf_op | source)
XLA Modules:
  0.0 57.2 jit_solution(631937509291436708)
XLA Ops:
  0.7 53.7 %waves.1 = (f32[2,2,256,128]{3,2,1,0:T(8,128)}, bf16[2,2,256,128]{3,2,1,0:T(8,128)(2,1)}, bf16[2,2,2,2,256,128]{5,4,3,2,1,0:T(8,128)(2,1)}, s32[2,8,128]{2,1,0:T(8,128)}) custom-call(s32[4]{0:T(128)} %rows.3, s32[4]{0:T(128)} %cols.1, s32[1]{0:T(128)S(6)} %copy.12.counts, s32[4]{0:T(128)} %dataset.1, f32[16]{0:T(128)} %dose.1, f32[16]{0:T(128)} %ground.1, ...), custom_call_target="tpu_custom_call" | custom-call | tf_op jit(solution)/shard_map/waves/pallas_call | solution.py:532
  54.4 2.8 %combine.1 = f32[2,1024,128]{2,1,0:T(8,128)} custom-call(s32[4]{0:T(128)} %rows.3, s32[2,8,128]{2,1,0:T(8,128)} %get-tuple-element.9.places, f32[2,2,256,128]{3,2,1,0:T(8,128)} %get-tuple-element.10.mine, bf16[2,2,256,128]{3,2,1,0:T(8,128)(2,1)} %get-tuple-element.11.theirs, bf16[2,2,2,2,256,128]{5,4,3,2,1,0:T(8,128)(2,1)} %get-tuple-element.12.halo), custom_call_target="tpu_custom_call" | custom-call | tf_op jit(solution)/shard_map/combine/pallas_call | solution.py:628

commit v3 on v2

--- a/solution.py
+++ b/solution.py
@@ -110,19 +110,23 @@
     lax.fori_loop(0, MODES, one, 0)
 
 
-def widen(halo, wide):
+def widen(halo, wide, takes):
     for side in range(2):
-        for c in range(2):
-            wide[side, c] = halo[side, c].astype(F32)
-
-
-def load_patch(own, wide, o_ref, place, row, col, first, last):
+        @pl.when(takes[side])
+        def _():
+            for c in range(2):
+                wide[side, c] = halo[side, c].astype(F32)
+
+        @pl.when(jnp.logical_not(takes[side]))
+        def _():
+            wide[side] = jnp.zeros((2, ROWS, Q), F32)
+
+
+def load_patch(own, wide, o_ref, place, row, col):
     lane = lax.broadcasted_iota(jnp.int32, (L, Q), 1)
     right = lane < col
-    empty = jnp.where(right, last, first) > 0
     for c in range(2):
-        halo = jnp.where(right, wide[1, c, pl.ds(row, L), :], wide[0, c, pl.ds(row, L), :])
-        o_ref[place, c, :, 0:Q] = jnp.where(empty, 0.0, halo)
+        o_ref[place, c, :, 0:Q] = jnp.where(right, wide[1, c, pl.ds(row, L), :], wide[0, c, pl.ds(row, L), :])
         o_ref[place, c, :, Q:L] = own[c, pl.ds(row, L), :]
 
 
@@ -304,11 +308,12 @@
 
 
 CHUNKS = 4
+RELEASE = 2
 MESH = pl.DeviceIdType.MESH
 
 
 def wave_kernel(
-    rows, cols, counts, dataset, dose, ground,
+    rows_in, cols_in, counts_in, dataset_in, dose_in, ground_in,
     trans, probe_in, measured_in, table_in, split_in,
     own_mine, own_in, halo_in, places_in,
     own_a, own_b, halo_a, halo_b, short, places, own_out, halo_out,
@@ -316,6 +321,7 @@
     o_ref, pr_ref, psi_ref, far_ref, int_ref, fac_ref, amp_ref, z, u, w, gz, grad_ref, wide,
     load_sem, own_send, own_recv, side_send, side_recv, relay_send, relay_recv,
     place_send, place_recv, grad_send, grad_recv, part_send, part_recv, go,
+    rows, cols, counts, dataset, dose, ground, small_sem,
 ):
     depth = lax.axis_index("depth")
     tile = lax.axis_index("tile")
@@ -324,9 +330,16 @@
     other = 1 - depth
     beside = (ahead, behind)
 
+    upper, lower = tile < tiles - 1, tile > 0
+    sends, takes = (upper, lower), (lower, upper)
+
     barrier = pltpu.get_barrier_semaphore()
-    for target in ((ahead, depth), (behind, depth), (ahead, other), (behind, other), (tile, other)):
-        pl.semaphore_signal(barrier, inc=1, device_id=target, device_id_type=MESH)
+    pl.semaphore_signal(barrier, inc=1, device_id=(tile, other), device_id_type=MESH)
+    for side in range(2):
+        @pl.when(sends[side])
+        def _():
+            for core in (depth, other):
+                pl.semaphore_signal(barrier, inc=1, device_id=(beside[side], core), device_id_type=MESH)
 
     def remote(src, dst, send, recv, target):
         return pltpu.make_async_remote_copy(
@@ -384,104 +397,114 @@
         @pl.when(depth == d)
         def _():
             own_load(mine[d][0]).start()
-    for load in loads:
+    smalls = [
+        pltpu.make_async_copy(src, dst, small_sem.at[n])
+        for n, (src, dst) in enumerate(
+            (
+                (rows_in, rows), (cols_in, cols), (counts_in, counts),
+                (dataset_in, dataset), (dose_in, dose), (ground_in, ground),
+            )
+        )
+    ]
+    for load in smalls + loads:
         load.start()
+    for d in range(2):
+        @pl.when(depth == d)
+        def _():
+            own_load(mine[d][0]).wait()
+            for c in range(2):
+                short[c] = mine[d][0][c].astype(BF)
+    pl.semaphore_wait(barrier, 1 + 2 * (lower.astype(jnp.int32) + upper.astype(jnp.int32)))
+
+    def sides(flags, act):
+        for side in range(2):
+            @pl.when(flags[side])
+            def _():
+                act(side)
+
+    def send_tiles(ref):
+        for k in range(CHUNKS):
+            sides(sends, lambda side: side_copy(ref, side, k).start())
+
+    for d in range(2):
+        @pl.when(depth == d)
+        def _():
+            own_copy(mine[d][0]).start()
+    @pl.when(depth == 0)
+    def _():
+        send_tiles(halo_a)
+
+    def spot(p):
+        slot = depth * SLOTS + p
+        return slot, jnp.clip(rows[slot], 0, ROWS - L), jnp.clip(cols[slot], 0, Q - 1)
+
+    for load in smalls:
+        load.wait()
     for n in range(4):
         places[n : n + 1, :] = jnp.full((1, Q), rows[n], jnp.int32)
         places[n + 4 : n + 5, :] = jnp.full((1, Q), cols[n], jnp.int32)
-    for d in range(2):
-        @pl.when(depth == d)
-        def _():
-            own_load(mine[d][0]).wait()
-            for c in range(2):
-                short[c] = mine[d][0][c].astype(BF)
-    pl.semaphore_wait(barrier, 5)
-
-    for d in range(2):
-        @pl.when(depth == d)
-        def _():
-            own_copy(mine[d][0]).start()
+    loads[0].wait()
+
+    def turn(p, _):
+        rotate_probe(probe, pr_ref, spin, p, spot(p)[2])
+        return 0
+
+    lax.fori_loop(0, SLOTS, turn, 0)
+    for load in loads[1:]:
+        load.wait()
+
+    def take(side, k, ref):
+        side_copy(ref, side, k).wait_recv()
+        relay_copy(ref, side, k).start()
+
+    @pl.when(depth == 0)
+    def _():
+        for k in range(RELEASE):
+            sides(sends, lambda side: side_copy(halo_a, side, k).wait_send())
+        pl.semaphore_signal(go, inc=1, device_id=(tile, other), device_id_type=MESH)
+        for k in range(CHUNKS):
+            sides(takes, lambda side: take(side, k, halo_a))
+        for k in range(RELEASE, CHUNKS):
+            sides(sends, lambda side: side_copy(halo_a, side, k).wait_send())
+        own_copy(own_b).wait_recv()
+
+    @pl.when(depth == 1)
+    def _():
+        pl.semaphore_wait(go, 1)
+        send_tiles(halo_b)
+        own_copy(own_a).wait_recv()
+        for k in range(CHUNKS):
+            sides(takes, lambda side: relay_copy(halo_a, side, k).wait_recv())
+    own_copy(own_a).wait_send()
+    sides(sends, lambda side: place_copy(side).start())
+    widen(halo_a, wide, takes)
+
+    def start(p, _):
+        _, row, col = spot(p)
+        load_patch(own_a, wide, o_ref, 2 * p, row, col)
+        forward_first(table, pr_ref, o_ref, p, z, u, w, psi_ref)
+
+        @pl.when(depth == 1)
+        def _():
+            for kk in range(CHUNKS // SLOTS):
+                sides(takes, lambda side: take(side, p * (CHUNKS // SLOTS) + kk, halo_b))
+        return 0
+
+    lax.fori_loop(0, SLOTS, start, 0)
+
     @pl.when(depth == 0)
     def _():
         for k in range(CHUNKS):
-            for side in range(2):
-                side_copy(halo_a, side, k).start()
-    for side in range(2):
-        place_copy(side).start()
-
-    def spot(p):
-        slot = depth * SLOTS + p
-        return slot, jnp.clip(rows[slot], 0, ROWS - L), jnp.clip(cols[slot], 0, Q - 1)
-
-    loads[0].wait()
-
-    def turn(p, _):
-        rotate_probe(probe, pr_ref, spin, p, spot(p)[2])
-        return 0
-
-    lax.fori_loop(0, SLOTS, turn, 0)
-    for load in loads[1:]:
-        load.wait()
-
-    @pl.when(depth == 0)
-    def _():
-        for k in range(CHUNKS):
-            for side in range(2):
-                side_copy(halo_a, side, k).wait_recv()
-                relay_copy(halo_a, side, k).start()
-        for k in range(CHUNKS):
-            for side in range(2):
-                side_copy(halo_a, side, k).wait_send()
-        pl.semaphore_signal(go, inc=1, device_id=(tile, other), device_id_type=MESH)
-        own_copy(own_b).wait_recv()
-
-    @pl.when(depth == 1)
-    def _():
-        pl.semaphore_wait(go, 1)
-        for k in range(CHUNKS):
-            for side in range(2):
-                side_copy(halo_b, side, k).start()
-        own_copy(own_a).wait_recv()
-        for k in range(CHUNKS):
-            for side in range(2):
-                relay_copy(halo_a, side, k).wait_recv()
-    own_copy(own_a).wait_send()
-    widen(halo_a, wide)
-
-    first = (tile == 0).astype(jnp.int32)
-    last = (tile == tiles - 1).astype(jnp.int32)
-
-    def start(p, _):
-        _, row, col = spot(p)
-        load_patch(own_a, wide, o_ref, 2 * p, row, col, first, last)
-        forward_first(table, pr_ref, o_ref, p, z, u, w, psi_ref)
-
-        @pl.when(depth == 1)
-        def _():
-            for kk in range(CHUNKS // SLOTS):
-                for side in range(2):
-                    k = p * (CHUNKS // SLOTS) + kk
-                    side_copy(halo_b, side, k).wait_recv()
-                    relay_copy(halo_b, side, k).start()
-        return 0
-
-    lax.fori_loop(0, SLOTS, start, 0)
-
-    @pl.when(depth == 0)
-    def _():
-        for k in range(CHUNKS):
-            for side in range(2):
-                relay_copy(halo_b, side, k).wait_recv()
-                relay_copy(halo_a, side, k).wait_send()
+            sides(takes, lambda side: relay_copy(halo_b, side, k).wait_recv())
+            sides(takes, lambda side: relay_copy(halo_a, side, k).wait_send())
 
     @pl.when(depth == 1)
     def _():
         for k in range(CHUNKS):
-            for side in range(2):
-                side_copy(halo_b, side, k).wait_send()
-                relay_copy(halo_b, side, k).wait_send()
-
-    widen(halo_b, wide)
+            sides(sends, lambda side: side_copy(halo_b, side, k).wait_send())
+            sides(takes, lambda side: relay_copy(halo_b, side, k).wait_send())
+
+    widen(halo_b, wide, takes)
 
     def hand_over(p, s):
         place = 2 * p + s
@@ -489,20 +512,18 @@
         def _():
             own_mine[p] = grad_ref[place, :, :, Q:L]
             halo_out[p, 0] = grad_ref[place, :, :, 0:Q].astype(BF)
-            for side in range(2):
-                grad_copy(p, 0, side).start()
+            sides(sends, lambda side: grad_copy(p, 0, side).start())
         @pl.when(depth != s)
         def _():
             own_out[p] = grad_ref[place, :, :, Q:L].astype(BF)
             halo_out[p, 1] = grad_ref[place, :, :, 0:Q].astype(BF)
-            for side in range(2):
-                grad_copy(p, 1, side).start()
+            sides(sends, lambda side: grad_copy(p, 1, side).start())
             part_copy(p).start()
 
     def finish(p, _):
         slot, row, col = spot(p)
         which = jnp.clip(dataset[slot], 0, dose.shape[0] - 1)
-        load_patch(own_b, wide, o_ref, 2 * p + 1, row, col, first, last)
+        load_patch(own_b, wide, o_ref, 2 * p + 1, row, col)
         amplitudes(measured, p, split, amp_ref, int_ref)
         forward_last(table, o_ref, p, z, u, psi_ref, far_ref, int_ref)
         residual_factor(int_ref, amp_ref, fac_ref, dose[which], ground[which], slot < counts[0])
@@ -514,15 +535,13 @@
 
     lax.fori_loop(0, SLOTS, finish, 0)
 
-    for side in range(2):
-        place_copy(side).wait()
+    sides(sends, lambda side: place_copy(side).wait_send())
+    sides(takes, lambda side: place_copy(side).wait_recv())
     for p in range(SLOTS):
         part_copy(p).wait()
-        for side in range(2):
-            for home in range(2):
-                grad_copy(p, home, side).wait_send()
-            for core in range(2):
-                grad_arrival(p, core, side).wait_recv()
+        for n in range(2):
+            sides(sends, lambda side: grad_copy(p, n, side).wait_send())
+            sides(takes, lambda side: grad_arrival(p, n, side).wait_recv())
 
 
 def waves(scalars, transmission, probe, measured):
@@ -537,7 +556,7 @@
             jax.ShapeDtypeStruct((2, 2, SLOTS, 2, L, Q), BF),
             jax.ShapeDtypeStruct((2, 8, Q), jnp.int32),
         ),
-        in_specs=[pl.BlockSpec(memory_space=SMEM)] * 6 + [hbm] * 5,
+        in_specs=[hbm] * 11,
         out_specs=(vm,) * 4,
         scratch_shapes=[
             VMEM((2, ROWS, Q), F32),
@@ -580,6 +599,13 @@
             dma((SLOTS,)),
             dma((SLOTS,)),
             pltpu.SemaphoreType.REGULAR,
+            SMEM((4,), jnp.int32),
+            SMEM((4,), jnp.int32),
+            SMEM((1,), jnp.int32),
+            SMEM((4,), jnp.int32),
+            SMEM((16,), F32),
+            SMEM((16,), F32),
+            dma((6,)),
         ],
         compiler_params=pltpu.CompilerParams(
             vmem_limit_bytes=60 * 2**20, collective_id=0, has_side_effects=True

time: 57.3 us -> 51.7 us (0.902)
  the two profiles are of different devices: /device:TPU:0 before, /device:TPU:96 now
where the time goes in v3:
time: 51.7 us; the launch traced here: 51.6 us
  Pallas kernels  50.9 us (98%)
  between operations  0.66 us (1%)
    pallas_call x1, Pallas kernels, waves(): pl.pallas_call(wave_kernel, out_shape=(jax.ShapeDtypeStruct((SLOTS, 2, L,...  48 us
    pallas_call x1, Pallas kernels, combine(): pl.pallas_call(combine_kernel, out_shape=jax.ShapeDtypeStruct((2, ROWS, Q...  2.89 us

profile of v3, /device:TPU:96, one launch (start us, length us, event | category | flops | bytes accessed | tf_op | source)
XLA Modules:
  0.0 51.6 jit_solution(13114128662206501648)
XLA Ops:
  0.7 48.0 %waves.1 = (f32[2,2,256,128]{3,2,1,0:T(8,128)}, bf16[2,2,256,128]{3,2,1,0:T(8,128)(2,1)}, bf16[2,2,2,2,256,128]{5,4,3,2,1,0:T(8,128)(2,1)}, s32[2,8,128]{2,1,0:T(8,128)}) custom-call(s32[4]{0:T(128)} %rows.1, s32[4]{0:T(128)} %cols_in.1, s32[1]{0:T(128)S(6)} %copy.12.counts_in, s32[4]{0:T(128)} %dataset_in.1, f32[16]{0:T(128)} %dose_in.1, f32[16]{0:T(128)} %ground_in.1, ...), custom_call_target="tpu_custom_call" | custom-call | tf_op jit(solution)/shard_map/waves/pallas_call | solution.py:551
  48.7 2.9 %combine.1 = f32[2,1024,128]{2,1,0:T(8,128)} custom-call(s32[4]{0:T(128)} %rows.1, s32[2,8,128]{2,1,0:T(8,128)} %get-tuple-element.9.places, f32[2,2,256,128]{3,2,1,0:T(8,128)} %get-tuple-element.10.mine, bf16[2,2,256,128]{3,2,1,0:T(8,128)(2,1)} %get-tuple-element.11.theirs, bf16[2,2,2,2,256,128]{5,4,3,2,1,0:T(8,128)(2,1)} %get-tuple-element.12.halo), custom_call_target="tpu_custom_call" | custom-call | tf_op jit(solution)/shard_map/combine/pallas_call | solution.py:654

commit v4 on v3

--- a/solution.py
+++ b/solution.py
@@ -12,7 +12,7 @@
 L = 256
 Q = 128
 MODES = 6
-GROUP = 3
+GROUP = 6
 SLOTS = 2
 ROWS = 1024
 BF = jnp.bfloat16
@@ -66,7 +66,7 @@
     return [[fn(i, j) for j in range(2)] for i in range(2)]
 
 
-CH = 16
+CH = 8
 
 
 def store_waves(z_ref, m, r, re, im):
@@ -139,7 +139,7 @@
         rest = x - hi.astype(F32)
         mid = rest.astype(BF)
         lo = (rest - mid.astype(F32)).astype(BF)
-        amp_ref[i] = dot(hi, split[...]) + (dot(mid, split[...]) + dot(lo, split[...]))
+        amp_ref[slot, i] = dot(hi, split[...]) + (dot(mid, split[...]) + dot(lo, split[...]))
 
 
 def forward_first(table, pr_ref, o_ref, p, z, u, w, psi_ref):
@@ -171,12 +171,10 @@
                         psi_ref[p, m, 1, rows, lanes] = vim[i][j].astype(BF)
         return 0
 
-    lax.fori_loop(0, MODES // GROUP, group, 0)
+    group(0, 0)
 
 
 def forward_last(table, o_ref, p, z, u, psi_ref, far_ref, int_ref):
-    int_ref[...] = jnp.zeros_like(int_ref)
-
     def group(g, _):
         for k in range(GROUP):
             m = g * GROUP + k
@@ -197,38 +195,41 @@
                 far_ref[g * GROUP + k, j] = dot(u[k, j], table[1, j, 1])
         for j in range(2):
             for r in range(0, L, CH):
-                total = int_ref[j, r : r + CH, :]
+                total = None
                 for k in range(GROUP):
                     x = far_ref[g * GROUP + k, j, r : r + CH, 0:Q]
                     y = far_ref[g * GROUP + k, j, r : r + CH, Q:L]
-                    total = total + (x * x + y * y)
+                    power = x * x + y * y
+                    total = power if total is None else total + power
                 int_ref[j, r : r + CH, :] = total
         return 0
 
-    lax.fori_loop(0, MODES // GROUP, group, 0)
-
-
-def residual_factor(int_ref, amp_ref, fac_ref, scale, offset, valid):
+    group(0, 0)
+
+
+def residual_factor(int_ref, amp_ref, p, fac_ref, scale, offset, valid):
     for j in range(2):
         for i in range(2):
             intensity = scale * int_ref[j, Q * i : Q * i + Q, :] + offset
-            ratio = amp_ref[i, :, Q * j : Q * j + Q] / jnp.sqrt(intensity)
+            ratio = amp_ref[p, i, :, Q * j : Q * j + Q] / jnp.sqrt(intensity)
             fac_ref[j, Q * i : Q * i + Q, :] = jnp.where(valid, scale * (1.0 - ratio), 0.0)
 
 
-def conj_terms(grad_ref, place, r, terms):
-    for i in range(2):
-        for j in range(2):
-            rows, lanes = slice(Q * i + r, Q * i + r + CH), slice(Q * j, Q * j + Q)
-            gre, gim = grad_ref[place, 0, rows, lanes], grad_ref[place, 1, rows, lanes]
-            a, b, x, y = terms(i, j, rows, lanes)
-            grad_ref[place, 0, rows, lanes] = gre + (a * x + b * y)
-            grad_ref[place, 1, rows, lanes] = gim + (a * y - b * x)
+def cells(r):
+    return [(i, j, slice(Q * i + r, Q * i + r + CH), slice(Q * j, Q * j + Q)) for i in range(2) for j in range(2)]
+
+
+def add_conj(sums, n, a, b, x, y):
+    gre, gim = a * x + b * y, a * y - b * x
+    sums[n] = (gre, gim) if sums[n] is None else (sums[n][0] + gre, sums[n][1] + gim)
+
+
+def store_sums(grad_ref, place, r, sums):
+    for n, (i, j, rows, lanes) in enumerate(cells(r)):
+        grad_ref[place, 0, rows, lanes], grad_ref[place, 1, rows, lanes] = sums[n]
 
 
 def backward_last(table, o_ref, p, z, u, w, psi_ref, far_ref, fac_ref, grad_ref, gz_ref):
-    grad_ref[2 * p + 1] = jnp.zeros((2, L, L), F32)
-
     def group(g, _):
         for k in range(GROUP):
             m = g * GROUP + k
@@ -249,33 +250,23 @@
             for r in range(0, Q, CH):
                 vre, vim = read_waves(w, k, r)
                 vre, vim = hadamard(vre), hadamard(vim)
-                conj_terms(
-                    grad_ref,
-                    2 * p + 1,
-                    r,
-                    lambda i, j, rows, lanes: (
-                        psi_ref[p, m, 0, rows, lanes].astype(F32),
-                        psi_ref[p, m, 1, rows, lanes].astype(F32),
-                        vre[i][j],
-                        vim[i][j],
-                    ),
-                )
                 re, im = [[None] * 2 for _ in range(2)], [[None] * 2 for _ in range(2)]
-                for i in range(2):
-                    for j in range(2):
-                        rows, lanes = slice(Q * i + r, Q * i + r + CH), slice(Q * j, Q * j + Q)
-                        c, d = o_ref[2 * p + 1, 0, rows, lanes], o_ref[2 * p + 1, 1, rows, lanes]
-                        x, y = vre[i][j], vim[i][j]
-                        re[i][j], im[i][j] = c * x + d * y, c * y - d * x
+                for n, (i, j, rows, lanes) in enumerate(cells(r)):
+                    x, y = vre[i][j], vim[i][j]
+                    a, b = psi_ref[p, m, 0, rows, lanes].astype(F32), psi_ref[p, m, 1, rows, lanes].astype(F32)
+                    gre, gim = a * x + b * y, a * y - b * x
+                    if k > 0:
+                        gre, gim = grad_ref.at[2 * p + 1][0, rows, lanes] + gre, grad_ref.at[2 * p + 1][1, rows, lanes] + gim
+                    grad_ref.at[2 * p + 1][0, rows, lanes], grad_ref.at[2 * p + 1][1, rows, lanes] = gre, gim
+                    c, d = o_ref[2 * p + 1, 0, rows, lanes], o_ref[2 * p + 1, 1, rows, lanes]
+                    re[i][j], im[i][j] = c * x + d * y, c * y - d * x
                 store_waves(gz_ref, m, r, hadamard(re), hadamard(im))
         return 0
 
-    lax.fori_loop(0, MODES // GROUP, group, 0)
+    group(0, 0)
 
 
 def backward_first(table, pr_ref, p, u, w, grad_ref, gz_ref):
-    grad_ref[2 * p] = jnp.zeros((2, L, L), F32)
-
     def group(g, _):
         for k in range(GROUP):
             m = g * GROUP + k
@@ -286,25 +277,19 @@
                     u[k, j, Q * i : Q * i + Q, Q:L] = x[Q:L, Q * j : Q * j + Q]
         for k in range(GROUP):
             right_side(table, 0, 1, u, w, k)
-        for k in range(GROUP):
-            m = g * GROUP + k
-            for r in range(0, Q, CH):
+        for r in range(0, Q, CH):
+            sums = [None] * 4
+            for k in range(GROUP):
+                m = g * GROUP + k
                 vre, vim = read_waves(w, k, r)
                 vre, vim = hadamard(vre), hadamard(vim)
-                conj_terms(
-                    grad_ref,
-                    2 * p,
-                    r,
-                    lambda i, j, rows, lanes: (
-                        pr_ref[p, m, 0, rows, lanes],
-                        pr_ref[p, m, 1, rows, lanes],
-                        vre[i][j],
-                        vim[i][j],
-                    ),
-                )
-        return 0
-
-    lax.fori_loop(0, MODES // GROUP, group, 0)
+                for n, (i, j, rows, lanes) in enumerate(cells(r)):
+                    a, b = pr_ref[p, m, 0, rows, lanes], pr_ref[p, m, 1, rows, lanes]
+                    add_conj(sums, n, a, b, vre[i][j], vim[i][j])
+            store_sums(grad_ref, 2 * p, r, sums)
+        return 0
+
+    group(0, 0)
 
 
 CHUNKS = 4
@@ -443,15 +428,15 @@
     for n in range(4):
         places[n : n + 1, :] = jnp.full((1, Q), rows[n], jnp.int32)
         places[n + 4 : n + 5, :] = jnp.full((1, Q), cols[n], jnp.int32)
-    loads[0].wait()
+    for load in loads:
+        load.wait()
 
     def turn(p, _):
         rotate_probe(probe, pr_ref, spin, p, spot(p)[2])
+        amplitudes(measured, p, split, amp_ref, int_ref)
         return 0
 
     lax.fori_loop(0, SLOTS, turn, 0)
-    for load in loads[1:]:
-        load.wait()
 
     def take(side, k, ref):
         side_copy(ref, side, k).wait_recv()
@@ -524,9 +509,8 @@
         slot, row, col = spot(p)
         which = jnp.clip(dataset[slot], 0, dose.shape[0] - 1)
         load_patch(own_b, wide, o_ref, 2 * p + 1, row, col)
-        amplitudes(measured, p, split, amp_ref, int_ref)
         forward_last(table, o_ref, p, z, u, psi_ref, far_ref, int_ref)
-        residual_factor(int_ref, amp_ref, fac_ref, dose[which], ground[which], slot < counts[0])
+        residual_factor(int_ref, amp_ref, p, fac_ref, dose[which], ground[which], slot < counts[0])
         backward_last(table, o_ref, p, z, u, w, psi_ref, far_ref, fac_ref, grad_ref, gz)
         hand_over(p, 1)
         backward_first(table, pr_ref, p, u, w, grad_ref, gz)
@@ -578,7 +562,7 @@
             VMEM((MODES, 2, L, L), F32),
             VMEM((2, L, Q), F32),
             VMEM((2, L, Q), F32),
-            VMEM((2, Q, L), F32),
+            VMEM((SLOTS, 2, Q, L), F32),
             VMEM((GROUP, 2, L, L), BF),
             VMEM((GROUP, 2, L, L), BF),
             VMEM((GROUP, 2, L, L), F32),

time: 51.7 us -> 48 us (0.928)
  Pallas kernels: 50.9 us -> 47.2 us
    pallas_call x1, Pallas kernels: 48 us -> 44.3 us  [waves(): pl.pallas_call(wave_kernel, out_shape=(jax.ShapeDtypeStruct((SLOTS, 2, L,...]
where the time goes in v4:
time: 48 us; the launch traced here: 47.9 us
  Pallas kernels  47.2 us (98%)
  between operations  0.66 us (1%)
    pallas_call x1, Pallas kernels, waves(): pl.pallas_call(wave_kernel, out_shape=(jax.ShapeDtypeStruct((SLOTS, 2, L,...  44.3 us
    pallas_call x1, Pallas kernels, combine(): pl.pallas_call(combine_kernel, out_shape=jax.ShapeDtypeStruct((2, ROWS, Q...  2.89 us

profile of v4, /device:TPU:96, one launch (start us, length us, event | category | flops | bytes accessed | tf_op | source)
XLA Modules:
  0.0 47.9 jit_solution(12370592040966602156)
XLA Ops:
  0.7 44.3 %waves.1 = (f32[2,2,256,128]{3,2,1,0:T(8,128)}, bf16[2,2,256,128]{3,2,1,0:T(8,128)(2,1)}, bf16[2,2,2,2,256,128]{5,4,3,2,1,0:T(8,128)(2,1)}, s32[2,8,128]{2,1,0:T(8,128)}) custom-call(s32[4]{0:T(128)} %rows.1, s32[4]{0:T(128)} %cols_in.1, s32[1]{0:T(128)S(6)} %copy.12.counts_in, s32[4]{0:T(128)} %dataset_in.1, f32[16]{0:T(128)} %dose_in.1, f32[16]{0:T(128)} %ground_in.1, ...), custom_call_target="tpu_custom_call" | custom-call | tf_op jit(solution)/shard_map/waves/pallas_call | solution.py:535
  45.0 2.9 %combine.1 = f32[2,1024,128]{2,1,0:T(8,128)} custom-call(s32[4]{0:T(128)} %rows.1, s32[2,8,128]{2,1,0:T(8,128)} %get-tuple-element.9.places, f32[2,2,256,128]{3,2,1,0:T(8,128)} %get-tuple-element.10.mine, bf16[2,2,256,128]{3,2,1,0:T(8,128)(2,1)} %get-tuple-element.11.theirs, bf16[2,2,2,2,256,128]{5,4,3,2,1,0:T(8,128)(2,1)} %get-tuple-element.12.halo), custom_call_target="tpu_custom_call" | custom-call | tf_op jit(solution)/shard_map/combine/pallas_call | solution.py:638

commit v5 on v4

--- a/solution.py
+++ b/solution.py
@@ -167,8 +167,8 @@
                 for i in range(2):
                     for j in range(2):
                         rows, lanes = slice(Q * i + r, Q * i + r + CH), slice(Q * j, Q * j + Q)
-                        psi_ref[p, m, 0, rows, lanes] = vre[i][j].astype(BF)
-                        psi_ref[p, m, 1, rows, lanes] = vim[i][j].astype(BF)
+                        psi_ref[p, m, 0, rows, lanes] = vre[i][j]
+                        psi_ref[p, m, 1, rows, lanes] = vim[i][j]
         return 0
 
     group(0, 0)
@@ -183,8 +183,8 @@
                 for i in range(2):
                     for j in range(2):
                         rows, lanes = slice(Q * i + r, Q * i + r + CH), slice(Q * j, Q * j + Q)
-                        a = psi_ref[p, m, 0, rows, lanes].astype(F32)
-                        b = psi_ref[p, m, 1, rows, lanes].astype(F32)
+                        a = psi_ref[p, m, 0, rows, lanes]
+                        b = psi_ref[p, m, 1, rows, lanes]
                         c, d = o_ref[2 * p + 1, 0, rows, lanes], o_ref[2 * p + 1, 1, rows, lanes]
                         re[i][j], im[i][j] = a * c - b * d, a * d + b * c
                 store_waves(z, k, r, hadamard(re), hadamard(im))
@@ -253,7 +253,7 @@
                 re, im = [[None] * 2 for _ in range(2)], [[None] * 2 for _ in range(2)]
                 for n, (i, j, rows, lanes) in enumerate(cells(r)):
                     x, y = vre[i][j], vim[i][j]
-                    a, b = psi_ref[p, m, 0, rows, lanes].astype(F32), psi_ref[p, m, 1, rows, lanes].astype(F32)
+                    a, b = psi_ref[p, m, 0, rows, lanes], psi_ref[p, m, 1, rows, lanes]
                     gre, gim = a * x + b * y, a * y - b * x
                     if k > 0:
                         gre, gim = grad_ref.at[2 * p + 1][0, rows, lanes] + gre, grad_ref.at[2 * p + 1][1, rows, lanes] + gim
@@ -293,7 +293,7 @@
 
 
 CHUNKS = 4
-RELEASE = 2
+RELEASE = 3
 MESH = pl.DeviceIdType.MESH
 
 
@@ -495,14 +495,14 @@
         place = 2 * p + s
         @pl.when(depth == s)
         def _():
-            own_mine[p] = grad_ref[place, :, :, Q:L]
             halo_out[p, 0] = grad_ref[place, :, :, 0:Q].astype(BF)
             sides(sends, lambda side: grad_copy(p, 0, side).start())
+            own_mine[p] = grad_ref[place, :, :, Q:L]
         @pl.when(depth != s)
         def _():
-            own_out[p] = grad_ref[place, :, :, Q:L].astype(BF)
             halo_out[p, 1] = grad_ref[place, :, :, 0:Q].astype(BF)
             sides(sends, lambda side: grad_copy(p, 1, side).start())
+            own_out[p] = grad_ref[place, :, :, Q:L].astype(BF)
             part_copy(p).start()
 
     def finish(p, _):
@@ -558,7 +558,7 @@
             VMEM((L, L), BF),
             VMEM((4, 2, L, L), F32),
             VMEM((SLOTS, MODES, 2, L, L), F32),
-            VMEM((SLOTS, MODES, 2, L, L), BF),
+            VMEM((SLOTS, MODES, 2, L, L), F32),
             VMEM((MODES, 2, L, L), F32),
             VMEM((2, L, Q), F32),
             VMEM((2, L, Q), F32),
@@ -640,7 +640,7 @@
         out_shape=jax.ShapeDtypeStruct((2, ROWS, Q), F32),
         in_specs=[pl.BlockSpec(memory_space=SMEM)] * 2 + [vm] * 3,
         out_specs=vm,
-        compiler_params=pltpu.CompilerParams(vmem_limit_bytes=60 * 2**20),
+        compiler_params=pltpu.CompilerParams(vmem_limit_bytes=8 * 2**20),
         name="combine",
     )(rows, places, *parts)
 

time: 48 us -> 50.4 us (1.050)
  local copies, waits for them, and re-layouts: 0 us -> 3.91 us
  Pallas kernels: 47.2 us -> 45.5 us
    unnamed x0 -> x10, local copies, waits for them, and re-layouts: none -> 3.91 us
    pallas_call x1, Pallas kernels: 44.3 us -> 43.4 us  [waves(): pl.pallas_call(wave_kernel, out_shape=(jax.ShapeDtypeStruct((SLOTS, 2, L,...]
    pallas_call x1, Pallas kernels: 2.89 us -> 2.07 us  [combine(): pl.pallas_call(combine_kernel, out_shape=jax.ShapeDtypeStruct((2, ROWS, Q...]
where the time goes in v5:
time: 50.4 us; the launch traced here: 50.1 us
  Pallas kernels  45.5 us (90%)
  local copies, waits for them, and re-layouts  3.91 us (8%)
  between operations  0.69 us (1%)
    pallas_call x1, Pallas kernels, waves(): pl.pallas_call(wave_kernel, out_shape=(jax.ShapeDtypeStruct((SLOTS, 2, L,...  43.4 us
    unnamed x10, local copies, waits for them, and re-layouts  3.91 us
    pallas_call x1, Pallas kernels, combine(): pl.pallas_call(combine_kernel, out_shape=jax.ShapeDtypeStruct((2, ROWS, Q...  2.07 us

profile of v5, /device:TPU:96, one launch (start us, length us, event | category | flops | bytes accessed | tf_op | source)
XLA Modules:
  0.0 50.1 jit_solution(14378644693689013767)
XLA Ops:
  0.7 0.0 copy-start.4
  0.7 43.4 %waves.1 = (f32[2,2,256,128]{3,2,1,0:T(8,128)}, bf16[2,2,256,128]{3,2,1,0:T(8,128)(2,1)}, bf16[2,2,2,2,256,128]{5,4,3,2,1,0:T(8,128)(2,1)}, s32[2,8,128]{2,1,0:T(8,128)}) custom-call(s32[4]{0:T(128)} %rows.1, s32[4]{0:T(128)} %cols_in.1, s32[1]{0:T(128)S(6)} %copy.12.counts_in, s32[4]{0:T(128)} %dataset_in.1, f32[16]{0:T(128)} %dose_in.1, f32[16]{0:T(128)} %ground_in.1, ...), custom_call_target="tpu_custom_call" | custom-call | tf_op jit(solution)/shard_map/waves/pallas_call | solution.py:535
  44.1 0.0 copy-done.4
  44.1 0.0 copy-start
  44.1 1.2 %copy-done = bf16[2,2,2,2,256,128]{5,4,3,2,1,0:T(8,128)(2,1)S(1)} copy-done((bf16[2,2,2,2,256,128]{5,4,3,2,1,0:T(8,128)(2,1)S(1)}, bf16[2,2,2,2,256,128]{5,4,3,2,1,0:T(8,128)(2,1)}, u32[]{:S(2)}) %copy-start) | copy-done | bytes 1048600
  45.3 0.0 copy-start.1
  45.3 1.0 %copy-done.1 = f32[2,2,256,128]{3,2,1,0:T(8,128)S(1)} copy-done((f32[2,2,256,128]{3,2,1,0:T(8,128)S(1)}, f32[2,2,256,128]{3,2,1,0:T(8,128)}, u32[]{:S(2)}) %copy-start.1) | copy-done | bytes 524312
  46.4 0.0 copy-start.2
  46.4 0.9 %copy-done.2 = bf16[2,2,256,128]{3,2,1,0:T(8,128)(2,1)S(1)} copy-done((bf16[2,2,256,128]{3,2,1,0:T(8,128)(2,1)S(1)}, bf16[2,2,256,128]{3,2,1,0:T(8,128)(2,1)}, u32[]{:S(2)}) %copy-start.2) | copy-done | bytes 262168
  47.3 0.0 copy-start.3
  47.3 0.7 %copy-done.3 = s32[2,8,128]{2,1,0:T(8,128)S(1)} copy-done((s32[2,8,128]{2,1,0:T(8,128)S(1)}, s32[2,8,128]{2,1,0:T(8,128)}, u32[]{:S(2)}) %copy-start.3) | copy-done | bytes 8216
  48.0 2.1 %combine.1 = f32[2,1024,128]{2,1,0:T(8,128)} custom-call(s32[4]{0:T(128)S(1)} %copy-done.4, s32[2,8,128]{2,1,0:T(8,128)S(1)} %copy-done.3, f32[2,2,256,128]{3,2,1,0:T(8,128)S(1)} %copy-done.1, bf16[2,2,256,128]{3,2,1,0:T(8,128)(2,1)S(1)} %copy-done.2, bf16[2,2,2,2,256,128]{5,4,3,2,1,0:T(8,128)(2,1)S(1)} %copy-done), custom_call_target="tpu_custom_call" | custom-call | tf_op jit(solution)/shard_map/combine/pallas_call | solution.py:638
Async XLA Ops:
  0.7 43.4 %copy-start.4 = (s32[4]{0:T(128)S(1)}, s32[4]{0:T(128)}, u32[]{:S(2)}) copy-start(s32[4]{0:T(128)} %rows.1) | copy-start | bytes 52
  44.1 1.2 %copy-start = (bf16[2,2,2,2,256,128]{5,4,3,2,1,0:T(8,128)(2,1)S(1)}, bf16[2,2,2,2,256,128]{5,4,3,2,1,0:T(8,128)(2,1)}, u32[]{:S(2)}) copy-start(bf16[2,2,2,2,256,128]{5,4,3,2,1,0:T(8,128)(2,1)} %get-tuple-element.12.halo) | copy-start | bytes 3145732
  45.3 1.0 %copy-start.1 = (f32[2,2,256,128]{3,2,1,0:T(8,128)S(1)}, f32[2,2,256,128]{3,2,1,0:T(8,128)}, u32[]{:S(2)}) copy-start(f32[2,2,256,128]{3,2,1,0:T(8,128)} %get-tuple-element.10.mine) | copy-start | bytes 1572868
  46.4 0.9 %copy-start.2 = (bf16[2,2,256,128]{3,2,1,0:T(8,128)(2,1)S(1)}, bf16[2,2,256,128]{3,2,1,0:T(8,128)(2,1)}, u32[]{:S(2)}) copy-start(bf16[2,2,256,128]{3,2,1,0:T(8,128)(2,1)} %get-tuple-element.11.theirs) | copy-start | bytes 786436
  47.3 0.7 %copy-start.3 = (s32[2,8,128]{2,1,0:T(8,128)S(1)}, s32[2,8,128]{2,1,0:T(8,128)}, u32[]{:S(2)}) copy-start(s32[2,8,128]{2,1,0:T(8,128)} %get-tuple-element.9.places) | copy-start | bytes 24580

commit v6 on v5

--- a/solution.py
+++ b/solution.py
@@ -592,16 +592,21 @@
             dma((6,)),
         ],
         compiler_params=pltpu.CompilerParams(
-            vmem_limit_bytes=60 * 2**20, collective_id=0, has_side_effects=True
+            vmem_limit_bytes=48 * 2**20, collective_id=0, has_side_effects=True
         ),
         name="waves",
     )(
-        *scalars,
-        transmission,
-        probe,
-        measured,
-        jnp.asarray(tables()).astype(BF),
-        jnp.asarray(lane_split()).astype(BF),
+        *[
+            x if x.shape == (1,) else pltpu.with_memory_space_constraint(x, pltpu.HBM)
+            for x in (
+                *scalars,
+                transmission,
+                probe,
+                measured,
+                jnp.asarray(tables()).astype(BF),
+                jnp.asarray(lane_split()).astype(BF),
+            )
+        ]
     )
 
 

time: 50.4 us -> 45 us (0.89)
  local copies, waits for them, and re-layouts: 3.91 us -> 0.01 us
  Pallas kernels: 45.5 us -> 44.2 us
    unnamed x10 -> x2, local copies, waits for them, and re-layouts: 3.91 us -> 0.01 us
    pallas_call x1, Pallas kernels: 43.4 us -> 42.1 us  [waves(): pl.pallas_call(wave_kernel, out_shape=(jax.ShapeDtypeStruct((SLOTS, 2, L,...]
where the time goes in v6:
time: 45 us; the launch traced here: 44.9 us
  Pallas kernels  44.2 us (98%)
  between operations  0.68 us (2%)
    pallas_call x1, Pallas kernels, waves(): pl.pallas_call(wave_kernel, out_shape=(jax.ShapeDtypeStruct((SLOTS, 2, L,...  42.1 us
    pallas_call x1, Pallas kernels, combine(): pl.pallas_call(combine_kernel, out_shape=jax.ShapeDtypeStruct((2, ROWS, Q...  2.05 us

profile of v6, /device:TPU:96, one launch (start us, length us, event | category | flops | bytes accessed | tf_op | source)
XLA Modules:
  0.0 44.9 jit_solution(2357507784824079234)
XLA Ops:
  0.7 0.0 copy-start
  0.7 42.1 %waves.1 = (f32[2,2,256,128]{3,2,1,0:T(8,128)S(1)}, bf16[2,2,256,128]{3,2,1,0:T(8,128)(2,1)S(1)}, bf16[2,2,2,2,256,128]{5,4,3,2,1,0:T(8,128)(2,1)S(1)}, s32[2,8,128]{2,1,0:T(8,128)S(1)}) custom-call(s32[4]{0:T(128)} %rows.1, s32[4]{0:T(128)} %cols_in.1, s32[1]{0:T(128)S(6)} %copy.12.counts_in, s32[4]{0:T(128)} %dataset_in.1, f32[16]{0:T(128)} %dose_in.1, ...), custom_call_target="tpu_custom_call" | custom-call | tf_op jit(solution)/shard_map/waves/pallas_call | solution.py:535
  42.8 0.0 copy-done
  42.8 2.1 %combine.1 = f32[2,1024,128]{2,1,0:T(8,128)} custom-call(s32[4]{0:T(128)S(1)} %copy-done, s32[2,8,128]{2,1,0:T(8,128)S(1)} %get-tuple-element.9.places, f32[2,2,256,128]{3,2,1,0:T(8,128)S(1)} %get-tuple-element.10.mine, bf16[2,2,256,128]{3,2,1,0:T(8,128)(2,1)S(1)} %get-tuple-element.11.theirs, bf16[2,2,2,2,256,128]{5,4,3,2,1,0:T(8,128)(2,1)S(1)} %get-tuple-element.12.halo), custom_call_target="tpu_custom_call" | custom-call | tf_op jit(solution)/shard_map/combine/pallas_call | solution.py:643
Async XLA Ops:
  0.7 42.2 %copy-start = (s32[4]{0:T(128)S(1)}, s32[4]{0:T(128)}, u32[]{:S(2)}) copy-start(s32[4]{0:T(128)} %rows.1) | copy-start | bytes 52
